TPU v7x, 256 devices: a whole 4x4x8 slice. The times are simulated.
256 devices in a mesh: lon: 16 (over z, core), lat: 16 (over y, x).
Axes of the slice: x: 4, y: 4, z: 8, core: 2. Of those that a mesh axis runs over, the one named last changes fastest.
Arguments:
- wave_action: float32 [256, 128, 1152], P('lon', 'lat'), may hold values from -6 to 6
- lon_speed: float32 [256, 128, 1152], P('lon', 'lat'), may hold values from 4 to 128
- lat_speed: float32 [256, 128, 1152], P('lon', 'lat'), may hold values from 4 to 128
- land_mask: int32 [256, 128], P('lon', 'lat'), may hold values 0 or 1
- open_edges: int32 [2, 256], P(None, 'lon'), may hold values 0 or 1
Outputs:
- propagated: float32 [256, 128, 1152], P('lon', 'lat')
All inputs are finite; a program needn't handle non-finite values. No bound on the sum of `land_mask` or of `open_edges` on one device may be relied on, other than what follows from the above.
Results may differ from a plain program's by a relative error of at most 0.00002.
Values sent between devices are 32-bit elements; how exact they have to be, the bound alone decides.
No kernel may reach another device: no remote copies, remote signals or barrier semaphores. Data moves between devices by JAX's collectives and lax.ppermute only.
A program may use at most 64 MiB of HBM per device.

v0:
```python
import jax
import jax.numpy as jnp
from jax import lax
from jax.sharding import PartitionSpec as P

ND = 36


def shifted(block, axis, distance):
    devices = range(lax.axis_size(axis))
    route = [((i - distance) % len(devices), i) for i in devices]
    return lax.ppermute(block, axis, route)


def from_behind(value, axis, steps):
    count = lax.axis_size(axis)
    initial, last = (max(0, -steps), min(count, count - steps))
    return lax.ppermute(value, axis, [(source, source + steps) for source in range(initial, last)])


def bin_angles(bin_count):
    direction = jnp.arange(bin_count, dtype=jnp.int32) % ND
    heading = (direction.astype(jnp.float32) + 0.5) * (2.0 * jnp.pi / ND)
    return (jnp.cos(heading), jnp.sin(heading))


def upwind_parts(flow):
    return (jnp.maximum(flow, 0.0), jnp.maximum(-flow, 0.0))


def take_row(array, row_index, line_axis):
    return lax.index_in_dim(array, row_index, line_axis, keepdims=False)


def local_rows(bands, source, line_axis):
    lower_band, main_band, upper_band = bands
    row_count = source.shape[line_axis] - 1
    zeros_row = jnp.zeros_like(take_row(source, 0, line_axis))
    ratios = []
    forward = []
    ratio_prev = zeros_row
    state_prev = (zeros_row, zeros_row, zeros_row)
    for row_index in range(row_count):
        sub_row = take_row(lower_band, row_index, line_axis)
        main_row = take_row(main_band, row_index, line_axis)
        super_row = take_row(upper_band, row_index, line_axis)
        pivot = main_row - sub_row * ratio_prev
        left_term = -sub_row if row_index == 0 else zeros_row
        right_term = -super_row if row_index == row_count - 1 else zeros_row
        state_prev = (
            (take_row(source, row_index, line_axis) - sub_row * state_prev[0]) / pivot,
            (left_term - sub_row * state_prev[1]) / pivot,
            (right_term - sub_row * state_prev[2]) / pivot,
        )
        ratio_prev = super_row / pivot
        ratios.append(ratio_prev)
        forward.append(state_prev)
    state_next = forward[row_count - 1]
    solved = [state_next]
    for row_index in range(row_count - 2, -1, -1):
        state_next = tuple(
            (
                current - ratios[row_index] * further
                for current, further in zip(forward[row_index], state_next)
            )
        )
        solved.insert(0, state_next)
    return tuple(
        (jnp.stack([solved_row[member] for solved_row in solved], line_axis) for member in range(3))
    )


def interface_rows(bands, source, solved, incoming, line_axis):
    lower_band, main_band, upper_band = bands
    last_row = source.shape[line_axis] - 1
    sub_coef = take_row(lower_band, last_row, line_axis)
    main_coef = take_row(main_band, last_row, line_axis)
    super_coef = take_row(upper_band, last_row, line_axis)
    inner_rows = [take_row(solved_part, last_row - 1, line_axis) for solved_part in solved]
    sub_coupling = sub_coef * inner_rows[1]
    diagonal = main_coef + sub_coef * inner_rows[2] + super_coef * incoming[1]
    super_coupling = super_coef * incoming[2]
    reduced_rhs = (
        take_row(source, last_row, line_axis) - sub_coef * inner_rows[0] - super_coef * incoming[0]
    )
    return (sub_coupling, diagonal, super_coupling, reduced_rhs)


def normalize_rows(reduced):
    return jnp.stack([reduced[0] / reduced[1], reduced[2] / reduced[1], reduced[3] / reduced[1]], 0)


def combine_rows(scaled, from_below, from_above):
    diagonal = 1.0 - scaled[0] * from_below[1] - scaled[1] * from_above[0]
    return jnp.stack(
        [
            -scaled[0] * from_below[0] / diagonal,
            -scaled[1] * from_above[1] / diagonal,
            (scaled[2] - scaled[0] * from_below[2] - scaled[1] * from_above[2]) / diagonal,
        ],
        0,
    )


def assemble(solved, own_value, previous, line_axis):
    own_row = jnp.expand_dims(own_value, line_axis)
    prev_row = jnp.expand_dims(previous, line_axis)
    interior = solved[0] + solved[1] * prev_row + solved[2] * own_row
    return jnp.concatenate([interior, own_row], line_axis)


def body(wave_action, lon_speed, lat_speed, land_mask, open_edges):
    cosines, sine_terms = bin_angles(wave_action.shape[2])
    sea_mask = land_mask.astype(jnp.float32)[:, :, None]
    source = wave_action * sea_mask
    lon_flow = lon_speed * cosines * sea_mask
    onward, backward = upwind_parts(lon_flow)
    lon_bands = (-onward, 1.0 + onward + backward, -backward)
    solved = local_rows(lon_bands, source, 0)
    first_rows = jnp.stack([take_row(solved_part, 0, 0) for solved_part in solved], 0)
    incoming = shifted(first_rows, "lon", -1)
    reduced = interface_rows(lon_bands, source, solved, incoming, 0)
    scaled = normalize_rows(reduced)
    for doubling_bit in range(lax.axis_size("lon").bit_length() - 1):
        from_below = shifted(scaled, "lon", 1 << doubling_bit)
        from_above = shifted(scaled, "lon", -(1 << doubling_bit))
        scaled = combine_rows(scaled, from_below, from_above)
    own_value = scaled[2] / (1.0 + scaled[0] + scaled[1])
    previous = shifted(own_value, "lon", 1)
    halfway = assemble(solved, own_value, previous, 0)
    onward, backward = upwind_parts(lat_speed * sine_terms * sea_mask)
    opened = open_edges.astype(jnp.float32)
    row_place = lax.broadcasted_iota(jnp.int32, (1, halfway.shape[1], 1), 1)
    lat_place = lax.axis_index("lat")
    south_edge = jnp.logical_and(lat_place == 0, row_place == 0)
    north_edge = jnp.logical_and(
        lat_place == lax.axis_size("lat") - 1, row_place == halfway.shape[1] - 1
    )
    main_band = 1.0 + onward + backward
    main_band = jnp.where(south_edge, 1.0 + backward + onward * opened[0][:, None, None], main_band)
    main_band = jnp.where(north_edge, 1.0 + onward + backward * opened[1][:, None, None], main_band)
    lat_bands = (
        jnp.where(south_edge, 0.0, -onward),
        main_band,
        jnp.where(north_edge, 0.0, -backward),
    )
    solved = local_rows(lat_bands, halfway, 1)
    first_rows = jnp.stack([take_row(solved_part, 0, 1) for solved_part in solved], 0)
    incoming = from_behind(first_rows, "lat", -1)
    reduced = interface_rows(lat_bands, halfway, solved, incoming, 1)
    scaled = normalize_rows(reduced)
    for doubling_bit in range(lax.axis_size("lat").bit_length() - 1):
        from_below = from_behind(scaled, "lat", 1 << doubling_bit)
        from_above = from_behind(scaled, "lat", -(1 << doubling_bit))
        scaled = combine_rows(scaled, from_below, from_above)
    own_value = scaled[2] / (1.0 + scaled[0] + scaled[1])
    previous = from_behind(own_value, "lat", 1)
    return assemble(solved, own_value, previous, 1)


def solution(mesh):
    return jax.shard_map(
        body,
        mesh=mesh,
        in_specs=(
            P("lon", "lat", None),
            P("lon", "lat", None),
            P("lon", "lat", None),
            P("lon", "lat"),
            P(None, "lon"),
        ),
        out_specs=P("lon", "lat", None),
        check_vma=False,
    )
```

profile of v0, /device:TPU:2, one launch (start us, length us, event | category | flops | bytes accessed | tf_op | source)
XLA Modules:
  0.0 124.8 jit_solution(9674522766480510798)
XLA Ops:
  5.3 5.3 %collective-permute-start = (f32[3,8,1152]{2,1,0:T(8,128)S(1)}, f32[3,8,1152]{2,1,0:T(8,128)S(1)}, u32[]{:S(2)}, u32[]{:S(2)}) collective-permute-start(f32[3,8,1152]{2,1,0:T(8,128)S(1)} %pad_maximum_fusion.6), channel_id=1, source_target_pairs={{16,0},{32,16},{48,32},{64,48},{80,64},{96,80},{112,96},{128,112},... | collective-permute-start | bytes 331784 | tf_op jit(solution)/shard_map/ppermute | solution.py:12
  13.7 3.1 %collective-permute-start.2 = (f32[3,8,1152]{2,1,0:T(8,128)S(1)}, f32[3,8,1152]{2,1,0:T(8,128)S(1)}, u32[]{:S(2)}, u32[]{:S(2)}) collective-permute-start(f32[3,8,1152]{2,1,0:T(8,128)S(1)} %pad_maximum_fusion.7), channel_id=1, source_target_pairs={{16,0},{32,16},{48,32},{64,48},{80,64},{96,80},{112,96},{128,112},... | collective-permute-start | bytes 331784 | tf_op jit(solution)/shard_map/ppermute | solution.py:12
  16.8 2.4 %collective-permute-done.1 = f32[3,8,1152]{2,1,0:T(8,128)S(1)} collective-permute-done((f32[3,8,1152]{2,1,0:T(8,128)S(1)}, f32[3,8,1152]{2,1,0:T(8,128)S(1)}, u32[]{:S(2)}, u32[]{:S(2)}) %collective-permute-start.1) | collective-permute-done | bytes 110624 | tf_op jit(solution)/shard_map/ppermute | solution.py:12
  20.1 3.2 %collective-permute-start.4 = (f32[3,8,1152]{2,1,0:T(8,128)}, f32[3,8,1152]{2,1,0:T(8,128)}, u32[]{:S(2)}, u32[]{:S(2)}) collective-permute-start(f32[3,8,1152]{2,1,0:T(8,128)} %pad_maximum_fusion.8), channel_id=1, source_target_pairs={{32,0},{48,16},{64,32},{80,48},{96,64},{112,80},{128,96},{144,112}... | collective-permute-start | bytes 331784 | tf_op jit(solution)/shard_map/ppermute | solution.py:12
  23.3 3.6 %collective-permute-done.3 = f32[3,8,1152]{2,1,0:T(8,128)} collective-permute-done((f32[3,8,1152]{2,1,0:T(8,128)}, f32[3,8,1152]{2,1,0:T(8,128)}, u32[]{:S(2)}, u32[]{:S(2)}) %collective-permute-start.3) | collective-permute-done | bytes 110624 | tf_op jit(solution)/shard_map/ppermute | solution.py:12
  28.0 4.1 %collective-permute-start.6 = (f32[3,8,1152]{2,1,0:T(8,128)S(1)}, f32[3,8,1152]{2,1,0:T(8,128)S(1)}, u32[]{:S(2)}, u32[]{:S(2)}) collective-permute-start(f32[3,8,1152]{2,1,0:T(8,128)S(1)} %pad_maximum_fusion.9), channel_id=1, source_target_pairs={{64,0},{80,16},{96,32},{112,48},{128,64},{144,80},{160,96},{176,11... | collective-permute-start | bytes 331784 | tf_op jit(solution)/shard_map/ppermute | solution.py:12
  32.1 2.8 %collective-permute-done.5 = f32[3,8,1152]{2,1,0:T(8,128)S(1)} collective-permute-done((f32[3,8,1152]{2,1,0:T(8,128)S(1)}, f32[3,8,1152]{2,1,0:T(8,128)S(1)}, u32[]{:S(2)}, u32[]{:S(2)}) %collective-permute-start.5) | collective-permute-done | bytes 110624 | tf_op jit(solution)/shard_map/ppermute | solution.py:12
  36.3 3.8 %collective-permute-start.7 = (f32[3,8,1152]{2,1,0:T(8,128)S(1)}, f32[3,8,1152]{2,1,0:T(8,128)S(1)}, u32[]{:S(2)}, u32[]{:S(2)}) collective-permute-start(f32[3,8,1152]{2,1,0:T(8,128)S(1)} %pad_maximum_fusion.10), channel_id=1, source_target_pairs={{128,0},{144,16},{160,32},{176,48},{192,64},{208,80},{224,96},{240... | collective-permute-start | bytes 331784 | tf_op jit(solution)/shard_map/ppermute | solution.py:12
  40.6 4.4 %collective-permute-done.7 = f32[3,8,1152]{2,1,0:T(8,128)S(1)} collective-permute-done((f32[3,8,1152]{2,1,0:T(8,128)S(1)}, f32[3,8,1152]{2,1,0:T(8,128)S(1)}, u32[]{:S(2)}, u32[]{:S(2)}) %collective-permute-start.7) | collective-permute-done | bytes 110624 | tf_op jit(solution)/shard_map/ppermute | solution.py:12
  46.6 4.5 %collective-permute-done.8 = f32[8,1152]{1,0:T(8,128)S(1)} collective-permute-done((f32[8,1152]{1,0:T(8,128)S(1)}, f32[8,1152]{1,0:T(8,128)S(1)}, u32[]{:S(2)}, u32[]{:S(2)}) %collective-permute-start.8) | collective-permute-done | bytes 36896 | tf_op jit(solution)/shard_map/ppermute | solution.py:12
  52.2 2.4 %collective-permute-start.9 = (f32[3,16,1152]{2,1,0:T(8,128)S(1)}, f32[3,16,1152]{2,1,0:T(8,128)S(1)}, u32[]{:S(2)}, u32[]{:S(2)}) collective-permute-start(f32[3,16,1152]{2,1,0:T(8,128)S(1)} %pad_maximum_fusion.1), channel_id=1, source_target_pairs={{1,0},{2,1},{3,2},{4,3},{5,4},{6,5},{7,6},{8,7},{9,8},{10,9},{11,1... | collective-permute-start | bytes 663560 | tf_op jit(solution)/shard_map/ppermute | solution.py:18
  54.7 5.4 %collective-permute-done.9 = f32[3,16,1152]{2,1,0:T(8,128)S(1)} collective-permute-done((f32[3,16,1152]{2,1,0:T(8,128)S(1)}, f32[3,16,1152]{2,1,0:T(8,128)S(1)}, u32[]{:S(2)}, u32[]{:S(2)}) %collective-permute-start.9) | collective-permute-done | bytes 221216 | tf_op jit(solution)/shard_map/ppermute | solution.py:18
  60.2 3.4 %collective-permute-start.10 = (f32[3,16,1152]{2,1,0:T(8,128)S(1)}, f32[3,16,1152]{2,1,0:T(8,128)S(1)}, u32[]{:S(2)}, u32[]{:S(2)}) collective-permute-start(f32[3,16,1152]{2,1,0:T(8,128)S(1)} %pad_maximum_fusion.2), channel_id=1, source_target_pairs={{0,1},{1,2},{2,3},{3,4},{4,5},{5,6},{6,7},{7,8},{8,9},{9,10},{10,1... | collective-permute-start | bytes 663560 | tf_op jit(solution)/shard_map/ppermute | solution.py:18
  63.6 2.5 %collective-permute-start.11 = (f32[3,16,1152]{2,1,0:T(8,128)S(1)}, f32[3,16,1152]{2,1,0:T(8,128)S(1)}, u32[]{:S(2)}, u32[]{:S(2)}) collective-permute-start(f32[3,16,1152]{2,1,0:T(8,128)S(1)} %pad_maximum_fusion.2), channel_id=1, source_target_pairs={{1,0},{2,1},{3,2},{4,3},{5,4},{6,5},{7,6},{8,7},{9,8},{10,9},{11,1... | collective-permute-start | bytes 663560 | tf_op jit(solution)/shard_map/ppermute | solution.py:18
  68.1 4.7 %collective-permute-done.11 = f32[3,16,1152]{2,1,0:T(8,128)S(1)} collective-permute-done((f32[3,16,1152]{2,1,0:T(8,128)S(1)}, f32[3,16,1152]{2,1,0:T(8,128)S(1)}, u32[]{:S(2)}, u32[]{:S(2)}) %collective-permute-start.11) | collective-permute-done | bytes 221216 | tf_op jit(solution)/shard_map/ppermute | solution.py:18
  72.9 5.5 %collective-permute-start.12 = (f32[3,16,1152]{2,1,0:T(8,128)S(1)}, f32[3,16,1152]{2,1,0:T(8,128)S(1)}, u32[]{:S(2)}, u32[]{:S(2)}) collective-permute-start(f32[3,16,1152]{2,1,0:T(8,128)S(1)} %pad_maximum_fusion.3), channel_id=1, source_target_pairs={{0,2},{1,3},{2,4},{3,5},{4,6},{5,7},{6,8},{7,9},{8,10},{9,11},{10,... | collective-permute-start | bytes 663560 | tf_op jit(solution)/shard_map/ppermute | solution.py:18
  79.7 2.1 %collective-permute-done.12 = f32[3,16,1152]{2,1,0:T(8,128)S(1)} collective-permute-done((f32[3,16,1152]{2,1,0:T(8,128)S(1)}, f32[3,16,1152]{2,1,0:T(8,128)S(1)}, u32[]{:S(2)}, u32[]{:S(2)}) %collective-permute-start.12) | collective-permute-done | bytes 221216 | tf_op jit(solution)/shard_map/ppermute | solution.py:18
  81.8 5.9 %collective-permute-done.13 = f32[3,16,1152]{2,1,0:T(8,128)S(1)} collective-permute-done((f32[3,16,1152]{2,1,0:T(8,128)S(1)}, f32[3,16,1152]{2,1,0:T(8,128)S(1)}, u32[]{:S(2)}, u32[]{:S(2)}) %collective-permute-start.13) | collective-permute-done | bytes 221216 | tf_op jit(solution)/shard_map/ppermute | solution.py:18
  87.8 3.5 %collective-permute-start.14 = (f32[3,16,1152]{2,1,0:T(8,128)S(1)}, f32[3,16,1152]{2,1,0:T(8,128)S(1)}, u32[]{:S(2)}, u32[]{:S(2)}) collective-permute-start(f32[3,16,1152]{2,1,0:T(8,128)S(1)} %pad_maximum_fusion.4), channel_id=1, source_target_pairs={{0,4},{1,5},{2,6},{3,7},{4,8},{5,9},{6,10},{7,11},{8,12},{9,13},{1... | collective-permute-start | bytes 663560 | tf_op jit(solution)/shard_map/ppermute | solution.py:18
  92.6 2.1 %collective-permute-done.14 = f32[3,16,1152]{2,1,0:T(8,128)S(1)} collective-permute-done((f32[3,16,1152]{2,1,0:T(8,128)S(1)}, f32[3,16,1152]{2,1,0:T(8,128)S(1)}, u32[]{:S(2)}, u32[]{:S(2)}) %collective-permute-start.14) | collective-permute-done | bytes 221216 | tf_op jit(solution)/shard_map/ppermute | solution.py:18
  94.7 7.5 %collective-permute-done.15 = f32[3,16,1152]{2,1,0:T(8,128)S(1)} collective-permute-done((f32[3,16,1152]{2,1,0:T(8,128)S(1)}, f32[3,16,1152]{2,1,0:T(8,128)S(1)}, u32[]{:S(2)}, u32[]{:S(2)}) %collective-permute-start.15) | collective-permute-done | bytes 221216 | tf_op jit(solution)/shard_map/ppermute | solution.py:18
  102.2 4.8 %collective-permute-start.16 = (f32[3,16,1152]{2,1,0:T(8,128)S(1)}, f32[3,16,1152]{2,1,0:T(8,128)S(1)}, u32[]{:S(2)}, u32[]{:S(2)}) collective-permute-start(f32[3,16,1152]{2,1,0:T(8,128)S(1)} %pad_maximum_fusion.5), channel_id=1, source_target_pairs={{0,8},{1,9},{2,10},{3,11},{4,12},{5,13},{6,14},{7,15},{16,24},{17,... | collective-permute-start | bytes 663560 | tf_op jit(solution)/shard_map/ppermute | solution.py:18
  110.5 5.9 %collective-permute-done.17 = f32[3,16,1152]{2,1,0:T(8,128)S(1)} collective-permute-done((f32[3,16,1152]{2,1,0:T(8,128)S(1)}, f32[3,16,1152]{2,1,0:T(8,128)S(1)}, u32[]{:S(2)}, u32[]{:S(2)}) %collective-permute-start.17) | collective-permute-done | bytes 221216 | tf_op jit(solution)/shard_map/ppermute | solution.py:18
  121.4 2.2 %collective-permute-done.18 = f32[16,1152]{1,0:T(8,128)S(1)} collective-permute-done((f32[16,1152]{1,0:T(8,128)S(1)}, f32[16,1152]{1,0:T(8,128)S(1)}, u32[]{:S(2)}, u32[]{:S(2)}) %collective-permute-start.18) | collective-permute-done | bytes 73760 | tf_op jit(solution)/shard_map/ppermute | solution.py:18
  (198 shorter events, 28.5 us)
Async XLA Ops:
  3.3 9.7 %copy-start.14 = (f32[1,8,1152]{2,0,1:T(1,128)}, f32[1,8,1152]{2,0,1:T(1,128)S(1)}, u32[]{:S(2)}) copy-start(f32[1,8,1152]{2,0,1:T(1,128)S(1)} %get-tuple-element.203) | copy-start | bytes 110596
  5.3 7.6 %collective-permute-start = (f32[3,8,1152]{2,1,0:T(8,128)S(1)}, f32[3,8,1152]{2,1,0:T(8,128)S(1)}, u32[]{:S(2)}, u32[]{:S(2)}) collective-permute-start(f32[3,8,1152]{2,1,0:T(8,128)S(1)} %pad_maximum_fusion.6), channel_id=1, source_target_pairs={{16,0},{32,16},{48,32},{64,48},{80,64},{96,80},{112,96},{128,112},... | collective-permute-start | bytes 331784 | tf_op jit(solution)/shard_map/ppermute | solution.py:12
  13.0 7.0 %copy-start.1 = (f32[15,8,1152]{2,1,0:T(8,128)}, f32[15,8,1152]{2,1,0:T(8,128)S(1)}, u32[]{:S(2)}) copy-start(f32[15,8,1152]{2,1,0:T(8,128)S(1)} %get-tuple-element.244) | copy-start | bytes 1658884
  13.0 6.9 %copy-start.3 = (f32[15,8,1152]{2,1,0:T(8,128)}, f32[15,8,1152]{2,1,0:T(8,128)S(1)}, u32[]{:S(2)}) copy-start(f32[15,8,1152]{2,1,0:T(8,128)S(1)} %get-tuple-element.243) | copy-start | bytes 1658884
  13.7 5.5 %collective-permute-start.1 = (f32[3,8,1152]{2,1,0:T(8,128)S(1)}, f32[3,8,1152]{2,1,0:T(8,128)S(1)}, u32[]{:S(2)}, u32[]{:S(2)}) collective-permute-start(f32[3,8,1152]{2,1,0:T(8,128)S(1)} %pad_maximum_fusion.7), channel_id=1, source_target_pairs={{240,0},{0,16},{16,32},{32,48},{48,64},{64,80},{80,96},{96,112},{1... | collective-permute-start | bytes 331784 | tf_op jit(solution)/shard_map/ppermute | solution.py:12
  13.7 5.5 %collective-permute-start.2 = (f32[3,8,1152]{2,1,0:T(8,128)S(1)}, f32[3,8,1152]{2,1,0:T(8,128)S(1)}, u32[]{:S(2)}, u32[]{:S(2)}) collective-permute-start(f32[3,8,1152]{2,1,0:T(8,128)S(1)} %pad_maximum_fusion.7), channel_id=1, source_target_pairs={{16,0},{32,16},{48,32},{64,48},{80,64},{96,80},{112,96},{128,112},... | collective-permute-start | bytes 331784 | tf_op jit(solution)/shard_map/ppermute | solution.py:12
  20.0 6.9 %collective-permute-start.3 = (f32[3,8,1152]{2,1,0:T(8,128)}, f32[3,8,1152]{2,1,0:T(8,128)}, u32[]{:S(2)}, u32[]{:S(2)}) collective-permute-start(f32[3,8,1152]{2,1,0:T(8,128)} %pad_maximum_fusion.8), channel_id=1, source_target_pairs={{224,0},{240,16},{0,32},{16,48},{32,64},{48,80},{64,96},{80,112},{... | collective-permute-start | bytes 331784 | tf_op jit(solution)/shard_map/ppermute | solution.py:12
  20.1 6.9 %collective-permute-start.4 = (f32[3,8,1152]{2,1,0:T(8,128)}, f32[3,8,1152]{2,1,0:T(8,128)}, u32[]{:S(2)}, u32[]{:S(2)}) collective-permute-start(f32[3,8,1152]{2,1,0:T(8,128)} %pad_maximum_fusion.8), channel_id=1, source_target_pairs={{32,0},{48,16},{64,32},{80,48},{96,64},{112,80},{128,96},{144,112}... | collective-permute-start | bytes 331784 | tf_op jit(solution)/shard_map/ppermute | solution.py:12
  27.9 7.0 %collective-permute-start.5 = (f32[3,8,1152]{2,1,0:T(8,128)S(1)}, f32[3,8,1152]{2,1,0:T(8,128)S(1)}, u32[]{:S(2)}, u32[]{:S(2)}) collective-permute-start(f32[3,8,1152]{2,1,0:T(8,128)S(1)} %pad_maximum_fusion.9), channel_id=1, source_target_pairs={{192,0},{208,16},{224,32},{240,48},{0,64},{16,80},{32,96},{48,112}... | collective-permute-start | bytes 331784 | tf_op jit(solution)/shard_map/ppermute | solution.py:12
  28.0 8.2 %collective-permute-start.6 = (f32[3,8,1152]{2,1,0:T(8,128)S(1)}, f32[3,8,1152]{2,1,0:T(8,128)S(1)}, u32[]{:S(2)}, u32[]{:S(2)}) collective-permute-start(f32[3,8,1152]{2,1,0:T(8,128)S(1)} %pad_maximum_fusion.9), channel_id=1, source_target_pairs={{64,0},{80,16},{96,32},{112,48},{128,64},{144,80},{160,96},{176,11... | collective-permute-start | bytes 331784 | tf_op jit(solution)/shard_map/ppermute | solution.py:12
  36.3 8.7 %collective-permute-start.7 = (f32[3,8,1152]{2,1,0:T(8,128)S(1)}, f32[3,8,1152]{2,1,0:T(8,128)S(1)}, u32[]{:S(2)}, u32[]{:S(2)}) collective-permute-start(f32[3,8,1152]{2,1,0:T(8,128)S(1)} %pad_maximum_fusion.10), channel_id=1, source_target_pairs={{128,0},{144,16},{160,32},{176,48},{192,64},{208,80},{224,96},{240... | collective-permute-start | bytes 331784 | tf_op jit(solution)/shard_map/ppermute | solution.py:12
  45.2 5.9 %copy-start.2 = (f32[15,8,1152]{2,1,0:T(8,128)S(1)}, f32[15,8,1152]{2,1,0:T(8,128)}, u32[]{:S(2)}) copy-start(f32[15,8,1152]{2,1,0:T(8,128)} %copy-done.1) | copy-start | bytes 1658884
  46.5 4.6 %collective-permute-start.8 = (f32[8,1152]{1,0:T(8,128)S(1)}, f32[8,1152]{1,0:T(8,128)S(1)}, u32[]{:S(2)}, u32[]{:S(2)}) collective-permute-start(f32[8,1152]{1,0:T(8,128)S(1)} %fusion.134), channel_id=1, source_target_pairs={{240,0},{0,16},{16,32},{32,48},{48,64},{64,80},{80,96},{96,112},{1... | collective-permute-start | bytes 110600 | tf_op jit(solution)/shard_map/ppermute | solution.py:12
  52.2 7.8 %collective-permute-start.9 = (f32[3,16,1152]{2,1,0:T(8,128)S(1)}, f32[3,16,1152]{2,1,0:T(8,128)S(1)}, u32[]{:S(2)}, u32[]{:S(2)}) collective-permute-start(f32[3,16,1152]{2,1,0:T(8,128)S(1)} %pad_maximum_fusion.1), channel_id=1, source_target_pairs={{1,0},{2,1},{3,2},{4,3},{5,4},{6,5},{7,6},{8,7},{9,8},{10,9},{11,1... | collective-permute-start | bytes 663560 | tf_op jit(solution)/shard_map/ppermute | solution.py:18
  60.2 7.8 %collective-permute-start.10 = (f32[3,16,1152]{2,1,0:T(8,128)S(1)}, f32[3,16,1152]{2,1,0:T(8,128)S(1)}, u32[]{:S(2)}, u32[]{:S(2)}) collective-permute-start(f32[3,16,1152]{2,1,0:T(8,128)S(1)} %pad_maximum_fusion.2), channel_id=1, source_target_pairs={{0,1},{1,2},{2,3},{3,4},{4,5},{5,6},{6,7},{7,8},{8,9},{9,10},{10,1... | collective-permute-start | bytes 663560 | tf_op jit(solution)/shard_map/ppermute | solution.py:18
  63.6 9.1 %collective-permute-start.11 = (f32[3,16,1152]{2,1,0:T(8,128)S(1)}, f32[3,16,1152]{2,1,0:T(8,128)S(1)}, u32[]{:S(2)}, u32[]{:S(2)}) collective-permute-start(f32[3,16,1152]{2,1,0:T(8,128)S(1)} %pad_maximum_fusion.2), channel_id=1, source_target_pairs={{1,0},{2,1},{3,2},{4,3},{5,4},{6,5},{7,6},{8,7},{9,8},{10,9},{11,1... | collective-permute-start | bytes 663560 | tf_op jit(solution)/shard_map/ppermute | solution.py:18
  72.9 8.9 %collective-permute-start.12 = (f32[3,16,1152]{2,1,0:T(8,128)S(1)}, f32[3,16,1152]{2,1,0:T(8,128)S(1)}, u32[]{:S(2)}, u32[]{:S(2)}) collective-permute-start(f32[3,16,1152]{2,1,0:T(8,128)S(1)} %pad_maximum_fusion.3), channel_id=1, source_target_pairs={{0,2},{1,3},{2,4},{3,5},{4,6},{5,7},{6,8},{7,9},{8,10},{9,11},{10,... | collective-permute-start | bytes 663560 | tf_op jit(solution)/shard_map/ppermute | solution.py:18
  78.4 9.3 %collective-permute-start.13 = (f32[3,16,1152]{2,1,0:T(8,128)S(1)}, f32[3,16,1152]{2,1,0:T(8,128)S(1)}, u32[]{:S(2)}, u32[]{:S(2)}) collective-permute-start(f32[3,16,1152]{2,1,0:T(8,128)S(1)} %pad_maximum_fusion.3), channel_id=1, source_target_pairs={{2,0},{3,1},{4,2},{5,3},{6,4},{7,5},{8,6},{9,7},{10,8},{11,9},{12,... | collective-permute-start | bytes 663560 | tf_op jit(solution)/shard_map/ppermute | solution.py:18
  87.8 6.9 %collective-permute-start.14 = (f32[3,16,1152]{2,1,0:T(8,128)S(1)}, f32[3,16,1152]{2,1,0:T(8,128)S(1)}, u32[]{:S(2)}, u32[]{:S(2)}) collective-permute-start(f32[3,16,1152]{2,1,0:T(8,128)S(1)} %pad_maximum_fusion.4), channel_id=1, source_target_pairs={{0,4},{1,5},{2,6},{3,7},{4,8},{5,9},{6,10},{7,11},{8,12},{9,13},{1... | collective-permute-start | bytes 663560 | tf_op jit(solution)/shard_map/ppermute | solution.py:18
  91.3 10.9 %collective-permute-start.15 = (f32[3,16,1152]{2,1,0:T(8,128)S(1)}, f32[3,16,1152]{2,1,0:T(8,128)S(1)}, u32[]{:S(2)}, u32[]{:S(2)}) collective-permute-start(f32[3,16,1152]{2,1,0:T(8,128)S(1)} %pad_maximum_fusion.4), channel_id=1, source_target_pairs={{4,0},{5,1},{6,2},{7,3},{8,4},{9,5},{10,6},{11,7},{12,8},{13,9},{1... | collective-permute-start | bytes 663560 | tf_op jit(solution)/shard_map/ppermute | solution.py:18
  102.2 8.2 %collective-permute-start.16 = (f32[3,16,1152]{2,1,0:T(8,128)S(1)}, f32[3,16,1152]{2,1,0:T(8,128)S(1)}, u32[]{:S(2)}, u32[]{:S(2)}) collective-permute-start(f32[3,16,1152]{2,1,0:T(8,128)S(1)} %pad_maximum_fusion.5), channel_id=1, source_target_pairs={{0,8},{1,9},{2,10},{3,11},{4,12},{5,13},{6,14},{7,15},{16,24},{17,... | collective-permute-start | bytes 663560 | tf_op jit(solution)/shard_map/ppermute | solution.py:18
  107.0 9.3 %collective-permute-start.17 = (f32[3,16,1152]{2,1,0:T(8,128)S(1)}, f32[3,16,1152]{2,1,0:T(8,128)S(1)}, u32[]{:S(2)}, u32[]{:S(2)}) collective-permute-start(f32[3,16,1152]{2,1,0:T(8,128)S(1)} %pad_maximum_fusion.5), channel_id=1, source_target_pairs={{8,0},{9,1},{10,2},{11,3},{12,4},{13,5},{14,6},{15,7},{24,16},{25,... | collective-permute-start | bytes 663560 | tf_op jit(solution)/shard_map/ppermute | solution.py:18
  110.5 9.2 %copy-start = (f32[3,16,1152]{2,1,0:T(8,128)}, f32[3,16,1152]{2,1,0:T(8,128)S(1)}, u32[]{:S(2)}) copy-start(f32[3,16,1152]{2,1,0:T(8,128)S(1)} %collective-permute-done.16) | copy-start | bytes 663556
  117.4 6.2 %collective-permute-start.18 = (f32[16,1152]{1,0:T(8,128)S(1)}, f32[16,1152]{1,0:T(8,128)S(1)}, u32[]{:S(2)}, u32[]{:S(2)}) collective-permute-start(f32[16,1152]{1,0:T(8,128)S(1)} %get-tuple-element.5), channel_id=1, source_target_pairs={{0,1},{1,2},{2,3},{3,4},{4,5},{5,6},{6,7},{7,8},{8,9},{9,10},{10,1... | collective-permute-start | bytes 221192 | tf_op jit(solution)/shard_map/ppermute | solution.py:18
  (38 other events, 110.3 us)
where the time goes:
time: 125 us
  waiting for transfers between devices  60.8 us (49%)
  starting transfers between devices  47.6 us (38%)
  other arithmetic  11.4 us (9%)
  local copies, waits for them, and re-layouts  3.89 us (3%)
    ppermute x10, waiting for transfers between devices, from_behind(): lax.ppermute(value, axis, [(source, source + steps) for source in range(i...  39.8 us
    ppermute x10, starting transfers between devices, from_behind(): lax.ppermute(value, axis, [(source, source + steps) for source in range(i...  27.9 us
    ppermute x9, waiting for transfers between devices, shifted(): return lax.ppermute(block, axis, route)  21 us
    ppermute x9, starting transfers between devices, shifted(): return lax.ppermute(block, axis, route)  19.7 us
    div x4, other arithmetic, body(): own_value = scaled[2] / (1.0 + scaled[0] + scaled[1])  2.6 us
  transfers between devices with their start and end apart: 19, of which 17 were waited for; matrix products, arithmetic and copies ran while one was open for 2% of the time, Pallas kernels for 0%

commit v1 on v0

v1 whole, which is shorter than its diff:
```python
import jax
import jax.numpy as jnp
import numpy as np
from jax import lax
from jax.experimental import pallas as pl
from jax.experimental.pallas import tpu as pltpu
from jax.sharding import PartitionSpec as P

ND = 36
HALF = ND // 2
LANES = 128
CHUNK = 3 * LANES


def bin_tables(bins):
    heading = ((np.arange(bins) % ND).astype(np.float32) + np.float32(0.5)) * np.float32(2.0 * np.pi / ND)
    cosines, sines = np.cos(heading), np.sin(heading)
    rows = [np.abs(cosines), np.abs(sines), cosines > 0, sines > 0]
    return np.stack([np.asarray(row, np.float32) for row in rows] + [np.zeros(bins, np.float32)] * 4)


def chunks(bins):
    step = CHUNK if bins % CHUNK == 0 else bins
    return [slice(start, start + step) for start in range(0, bins, step)]


def tiles_of(part):
    return range(part.start // LANES, part.stop // LANES)


def take(ref, rows, part, start, size, stride=1):
    picked = [ref[pl.ds(tile * rows + start, size, stride=stride), :] for tile in tiles_of(part)]
    return jnp.concatenate(picked, axis=1)


def put(ref, rows, part, start, value, stride=1):
    for n, tile in enumerate(tiles_of(part)):
        place = pl.ds(tile * rows + start, value.shape[0], stride=stride)
        ref[place, :] = value[:, n * LANES : (n + 1) * LANES]


def compose(first, second):
    return second[0] * first[0], second[0] * first[1] + second[1]


def lon_local(wave, speed, mask, table, message, partial, decay):
    count, lats = mask.shape
    rows = count * lats
    sea = mask[...].astype(jnp.float32).T
    for part in chunks(wave.shape[1]):
        cosine, east = table[0:1, part], table[2:3, part] > 0.5

        def row(i):
            water = sea[:, i : i + 1]
            flow = speed[i * lats : (i + 1) * lats, part] * cosine * water
            scale = 1.0 / (1.0 + flow)
            return flow * scale, wave[i * lats : (i + 1) * lats, part] * water * scale

        value = total = None
        for k in range(count):
            if k < count // 2:
                a_low, b_low = row(k)
                a_high, b_high = row(count - 1 - k)
                there = (count - 1 - k) * lats
                put(decay, rows, part, there, jnp.where(east, a_high, a_low))
                put(partial, rows, part, there, jnp.where(east, b_high, b_low))
                a, b = jnp.where(east, a_low, a_high), jnp.where(east, b_low, b_high)
            else:
                a = take(decay, rows, part, k * lats, lats)
                b = take(partial, rows, part, k * lats, lats)
            value = b if k == 0 else a * value + b
            total = a if k == 0 else a * total
            put(partial, rows, part, k * lats, value)
            put(decay, rows, part, k * lats, total)
        message[0:lats, part] = total
        message[lats : 2 * lats, part] = value


def lat_coefficients(speed, mask, edges, table, ratio, scaled, decay, rate, arrived):
    lons, count = mask.shape
    rows = lons * count
    parts = chunks(speed.shape[1])

    def copy(tile):
        lanes = pl.ds(tile * LANES, LANES)
        return pltpu.make_async_copy(
            speed.at[:, lanes], rate.at[pl.ds(tile * rows, rows), :], arrived.at[tile]
        )

    for part in parts:
        for tile in tiles_of(part):
            copy(tile).start()
    place, last = lax.axis_index("lat"), lax.axis_size("lat") - 1
    sea = mask[...].astype(jnp.float32)
    opened = edges[...].astype(jnp.float32).T
    south = jnp.where(place == 0, opened[:, 0:1], 1.0)
    north = jnp.where(place == last, opened[:, 1:2], 1.0)
    for part in parts:
        for tile in tiles_of(part):
            copy(tile).wait()
        sine, up = table[1:2, part], table[3:4, part] > 0.5
        flows = [
            take(rate, rows, part, j, lons, count) * sine * sea[:, j : j + 1] for j in range(count)
        ]
        total = None
        for k in range(count):
            flow = jnp.where(up, flows[k], flows[count - 1 - k])
            shown = flow * jnp.where(up, south, north) if k == 0 else flow
            scale = 1.0 / (1.0 + shown)
            a = flow * scale
            total = a if k == 0 else a * total
            put(ratio, rows, part, k * lons, a)
            put(scaled, rows, part, k * lons, scale)
            put(decay, rows, part, k * lons, total)


def ordered_group(own, received, place, positive):
    members = [own, *received]
    in_place = []
    for slot in range(4):
        value = members[0]
        for d in range(1, 4):
            hit = (place + 4 - slot) % 4 == d
            value = [jnp.where(hit, new, old) for new, old in zip(members[d], value)]
        in_place.append(value)
    swept = [
        [jnp.where(positive, low, high) for low, high in zip(in_place[slot], in_place[3 - slot])]
        for slot in range(4)
    ]
    prefixes = [[jnp.ones_like(own[0]), jnp.zeros_like(own[1])], swept[0]]
    prefixes.append(compose(swept[0], swept[1]))
    prefixes.append(compose(prefixes[2], swept[2]))
    whole = compose(prefixes[3], swept[3])

    def chosen(index):
        value = prefixes[0]
        for slot in range(1, 4):
            value = [jnp.where(index == slot, new, old) for new, old in zip(prefixes[slot], value)]
        return value

    before = [jnp.where(positive, low, high) for low, high in zip(chosen(place), chosen(3 - place))]
    return whole, before


def halves(ref, part):
    rows = ref.shape[0] // 2
    return [ref[0:rows, part], ref[rows : 2 * rows, part]]


def lon_group(own, first, second, third, table, whole, before):
    place = lax.axis_index("lon") % 4
    rows = own.shape[0] // 2
    for part in chunks(own.shape[1]):
        received = [halves(ref, part) for ref in (first, second, third)]
        total, prefix = ordered_group(halves(own, part), received, place, table[2:3, part] > 0.5)
        whole[0:rows, part], whole[rows : 2 * rows, part] = total
        before[0:rows, part], before[rows : 2 * rows, part] = prefix


def lon_finish(
    partial, decay, own, first, second, third, before, ratio, scaled, lat_decay, table,
    message, solved, half,
):
    lats, lons = own.shape[0] // 2, message.shape[0] // 2
    rows = lons * lats
    for part in chunks(own.shape[1]):
        east, up = table[2:3, part] > 0.5, table[3:4, part] > 0.5
        one, two, three = (halves(ref, part) for ref in (first, second, third))
        cycle = halves(own, part)
        cycle = compose(cycle, [jnp.where(east, x, y) for x, y in zip(three, one)])
        cycle = compose(cycle, two)
        cycle = compose(cycle, [jnp.where(east, x, y) for x, y in zip(one, three)])
        entering = cycle[1] / (1.0 - cycle[0])
        prefix = halves(before, part)
        entering = prefix[0] * entering + prefix[1]
        for k in range(lons // 2):
            low, high = k * lats, (lons - 1 - k) * lats
            a, b = (
                take(partial, rows, part, at, lats) + take(decay, rows, part, at, lats) * entering
                for at in (low, high)
            )
            put(half, rows, part, low, jnp.where(east, a, b))
            put(half, rows, part, high, jnp.where(east, b, a))
        lines = [take(half, rows, part, j, lons, lats) for j in range(lats)]
        value = None
        for k in range(lats):
            step = take(scaled, rows, part, k * lons, lons)
            step = step * jnp.where(up, lines[k], lines[lats - 1 - k])
            value = step if k == 0 else take(ratio, rows, part, k * lons, lons) * value + step
            put(solved, rows, part, k * lons, value)
        message[0:lons, part] = take(lat_decay, rows, part, (lats - 1) * lons, lons)
        message[lons : 2 * lons, part] = value


def lat_group(own, first, second, third, table, before, *messages):
    place = lax.axis_index("lat")
    rows = own.shape[0] // 2
    everything = slice(0, own.shape[1])
    received = [halves(ref, everything) for ref in (first, second, third)]
    up = table[3:4, :] > 0.5
    total, prefix = ordered_group(halves(own, everything), received, place % 4, up)
    before[0:rows], before[rows : 2 * rows] = prefix
    turned = pltpu.roll(total[1], HALF, 1)
    north, south = jnp.where(up, total[0], turned), jnp.where(up, turned, total[0])
    for d, message in enumerate(messages, 1):
        message[...] = jnp.where(place // 4 + d < 4, north, south)


def lat_finish(solved, decay, before, first, second, third, table, out, result, sent):
    lons, bins = before.shape[0] // 2, before.shape[1]
    rows = out.shape[0]
    count = rows // lons
    row = lax.axis_index("lat") // 4
    up = table[3:4, :] > 0.5
    one, two, three = ((ref[...], pltpu.roll(ref[...], bins - HALF, 1)) for ref in (first, second, third))
    entering = jnp.zeros_like(one[0])
    for d, low, high in ((3, three, one), (2, two, two), (1, one, three)):
        a, b = (jnp.where(up, x, y) for x, y in zip(low, high))
        reached = jnp.where(up, (row >= d).astype(jnp.float32), (row < 4 - d).astype(jnp.float32))
        entering = jnp.where(reached > 0.5, a * entering + b, entering)
    entering = before[0:lons] * entering + before[lons : 2 * lons]
    copies = []
    for part in chunks(bins):
        goes_up, inflow = up[:, part], entering[:, part]
        for k in range(count // 2):
            low, high = k * lons, (count - 1 - k) * lons
            a, b = (
                take(solved, rows, part, at, lons) + take(decay, rows, part, at, lons) * inflow
                for at in (low, high)
            )
            put(result, rows, part, k, jnp.where(goes_up, a, b), count)
            put(result, rows, part, count - 1 - k, jnp.where(goes_up, b, a), count)
        for tile in tiles_of(part):
            copy = pltpu.make_async_copy(
                result.at[pl.ds(tile * rows, rows), :],
                out.at[:, pl.ds(tile * LANES, LANES)],
                sent.at[tile],
            )
            copy.start()
            copies.append(copy)
    for copy in copies:
        copy.wait()


def run(kernel, shapes, *operands, scratch=(), far_inputs=(), far_outputs=()):
    here, away = pl.BlockSpec(memory_space=pltpu.VMEM), pl.BlockSpec(memory_space=pl.ANY)
    return pl.pallas_call(
        kernel,
        out_shape=[jax.ShapeDtypeStruct(shape, jnp.float32) for shape in shapes],
        in_specs=[away if n in far_inputs else here for n in range(len(operands))],
        out_specs=[away if n in far_outputs else here for n in range(len(shapes))],
        scratch_shapes=scratch,
        name=kernel.__name__,
    )(*operands)


def exchange(value, axis, near):
    def route(d):
        pairs = []
        for i in range(16):
            base, k = (i - i % 4, i % 4) if near else (i % 4, i // 4)
            source = (k - d) % 4
            pairs.append((base + source if near else base + 4 * source, i))
        return pairs

    values = value if isinstance(value, list) else [value] * 3
    return [lax.ppermute(item, axis, route(d)) for d, item in enumerate(values, 1)]


def body(wave_action, lon_speed, lat_speed, land_mask, open_edges):
    lons, lats, bins = wave_action.shape
    table = jnp.asarray(bin_tables(bins))
    flat = (lons * lats, bins)
    wave, speed, lat_rate = (x.reshape(flat) for x in (wave_action, lon_speed, lat_speed))
    small, large = (2 * lats, bins), (2 * lons, bins)

    tiled = (bins // LANES * lons * lats, LANES)
    buffer = pltpu.VMEM(tiled, jnp.float32)
    signals = pltpu.SemaphoreType.DMA((bins // LANES,))

    own, partial, decay = run(lon_local, [small, tiled, tiled], wave, speed, land_mask, table)
    near = exchange(own, "lon", True)
    ratio, scaled, lat_decay = run(
        lat_coefficients, [tiled] * 3, lat_rate, land_mask, open_edges, table,
        scratch=[buffer, signals], far_inputs=(0,),
    )
    whole, before = run(lon_group, [small, small], own, *near, table)
    far = exchange(whole, "lon", False)
    lat_own, solved = run(
        lon_finish, [large, tiled],
        partial, decay, whole, *far, before, ratio, scaled, lat_decay, table,
        scratch=[buffer],
    )
    near = exchange(lat_own, "lat", True)
    lat_before, *sends = run(lat_group, [large, *[(lons, bins)] * 3], lat_own, *near, table)
    far = exchange(list(sends), "lat", False)
    (out,) = run(
        lat_finish, [flat], solved, lat_decay, lat_before, *far, table,
        scratch=[buffer, signals], far_outputs=(0,),
    )
    return out.reshape(wave_action.shape)


def solution(mesh):
    return jax.shard_map(
        body,
        mesh=mesh,
        in_specs=(
            P("lon", "lat", None),
            P("lon", "lat", None),
            P("lon", "lat", None),
            P("lon", "lat"),
            P(None, "lon"),
        ),
        out_specs=P("lon", "lat", None),
        check_vma=False,
    )
```

time: 125 us -> 58.5 us (0.47)
  the two profiles are of different devices: /device:TPU:2 before, /device:TPU:24 now
where the time goes in v1:
time: 58.5 us; the launch traced here: 58.1 us
  waiting for transfers between devices  19.3 us (33%)
  starting transfers between devices  19.1 us (33%)
  Pallas kernels  15.2 us (26%)
  local copies, waits for them, and re-layouts  4.54 us (8%)
    ppermute x12, waiting for transfers between devices, exchange(): lax.ppermute(item, axis, route(d))  19.3 us
    ppermute x12, starting transfers between devices, exchange(): lax.ppermute(item, axis, route(d))  19.1 us
    pallas_call x6, Pallas kernels, run(): pl.pallas_call(kernel, out_shape=[jax.ShapeDtypeStruct(shape, jnp.float32...  15.2 us
    unnamed x25, local copies, waits for them, and re-layouts  4.54 us
  transfers between devices with their start and end apart: 12, of which 9 were waited for; matrix products, arithmetic and copies ran while one was open for 0% of the time, Pallas kernels for 6%

profile of v1, /device:TPU:24, one launch (start us, length us, event | category | flops | bytes accessed | tf_op | source)
XLA Modules:
  0.0 58.1 jit_solution(16910876043792793636)
XLA Ops:
  0.0 1.3 %copy.7.mask = s32[16,8]{1,0:T(8,128)} copy(s32[16,8]{0,1:T(8,128)} %param.9) | data formatting | bytes 1024 | tf_op args[3]
  1.3 2.7 %lon_local.1 = (f32[16,1152]{1,0:T(8,128)}, f32[1152,128]{1,0:T(8,128)}, f32[1152,128]{1,0:T(8,128)}) custom-call(f32[128,1152]{1,0:T(8,128)} %bitcast.4, f32[128,1152]{1,0:T(8,128)} %bitcast.5, s32[16,8]{1,0:T(8,128)} %copy.7.mask, f32[8,1152]{1,0:T(8,128)} %constant.2.clone.table), custom_call_target="tpu_custom_call" | custom-call | tf_op jit(solution)/shard_map/lon_local/pallas_call | solution.py:247
  4.0 1.4 %collective-permute-start.2 = (f32[16,1152]{1,0:T(8,128)}, f32[16,1152]{1,0:T(8,128)S(1)}, u32[]{:S(2)}, u32[]{:S(2)}) collective-permute-start(f32[16,1152]{1,0:T(8,128)} %get-tuple-element.21.own), channel_id=1, source_target_pairs={{16,0},{32,16},{48,32},{0,48},{80,64},{96,80},{112,96},{64,112},{1... | collective-permute-start | bytes 221192 | tf_op jit(solution)/shard_map/ppermute | solution.py:267
  6.2 2.1 %collective-permute-done.2.third = f32[16,1152]{1,0:T(8,128)S(1)} collective-permute-done((f32[16,1152]{1,0:T(8,128)}, f32[16,1152]{1,0:T(8,128)S(1)}, u32[]{:S(2)}, u32[]{:S(2)}) %collective-permute-start.2) | collective-permute-done | bytes 73760 | tf_op jit(solution)/shard_map/ppermute | solution.py:267
  8.3 2.5 %collective-permute-done.1.second = f32[16,1152]{1,0:T(8,128)S(1)} collective-permute-done((f32[16,1152]{1,0:T(8,128)}, f32[16,1152]{1,0:T(8,128)S(1)}, u32[]{:S(2)}, u32[]{:S(2)}) %collective-permute-start.1) | collective-permute-done | bytes 73760 | tf_op jit(solution)/shard_map/ppermute | solution.py:267
  12.0 1.7 %lon_group.1 = (f32[16,1152]{1,0:T(8,128)}, f32[16,1152]{1,0:T(8,128)}) custom-call(f32[16,1152]{1,0:T(8,128)} %get-tuple-element.21.own, f32[16,1152]{1,0:T(8,128)} %copy-done.11, f32[16,1152]{1,0:T(8,128)} %copy-done.10, f32[16,1152]{1,0:T(8,128)} %copy-done.9, f32[8,1152]{1,0:T(8,128)} %constant.2.clone.table), custom_call_target="tpu_custom_call" | custom-call | tf_op jit(solution)/shard_map/lon_group/pallas_call | solution.py:247
  13.7 5.9 %collective-permute-start.5 = (f32[16,1152]{1,0:T(8,128)}, f32[16,1152]{1,0:T(8,128)S(1)}, u32[]{:S(2)}, u32[]{:S(2)}) collective-permute-start(f32[16,1152]{1,0:T(8,128)} %get-tuple-element.22.own), channel_id=1, source_target_pairs={{64,0},{80,16},{96,32},{112,48},{128,64},{144,80},{160,96},{176,11... | collective-permute-start | bytes 221192 | tf_op jit(solution)/shard_map/ppermute | solution.py:267
  19.6 1.0 %collective-permute-start.4 = (f32[16,1152]{1,0:T(8,128)}, f32[16,1152]{1,0:T(8,128)S(1)}, u32[]{:S(2)}, u32[]{:S(2)}) collective-permute-start(f32[16,1152]{1,0:T(8,128)} %get-tuple-element.22.own), channel_id=1, source_target_pairs={{128,0},{144,16},{160,32},{176,48},{192,64},{208,80},{224,96},{240... | collective-permute-start | bytes 221192 | tf_op jit(solution)/shard_map/ppermute | solution.py:267
  20.6 2.8 %collective-permute-start.3 = (f32[16,1152]{1,0:T(8,128)}, f32[16,1152]{1,0:T(8,128)S(1)}, u32[]{:S(2)}, u32[]{:S(2)}) collective-permute-start(f32[16,1152]{1,0:T(8,128)} %get-tuple-element.22.own), channel_id=1, source_target_pairs={{192,0},{208,16},{224,32},{240,48},{0,64},{16,80},{32,96},{48,112}... | collective-permute-start | bytes 221192 | tf_op jit(solution)/shard_map/ppermute | solution.py:267
  23.4 3.3 %lat_coefficients.1 = (f32[1152,128]{1,0:T(8,128)}, f32[1152,128]{1,0:T(8,128)}, f32[1152,128]{1,0:T(8,128)}) custom-call(f32[128,1152]{1,0:T(8,128)} %bitcast.6, s32[16,8]{1,0:T(8,128)} %copy.7.mask, s32[2,16]{1,0:T(2,128)} %edges.1, f32[8,1152]{1,0:T(8,128)} %constant.2.clone.table), custom_call_target="tpu_custom_call" | custom-call | tf_op jit(solution)/shard_map/lat_coefficients/pallas_call | solution.py:247
  26.7 2.2 %collective-permute-done.4.second = f32[16,1152]{1,0:T(8,128)S(1)} collective-permute-done((f32[16,1152]{1,0:T(8,128)}, f32[16,1152]{1,0:T(8,128)S(1)}, u32[]{:S(2)}, u32[]{:S(2)}) %collective-permute-start.4) | collective-permute-done | bytes 73760 | tf_op jit(solution)/shard_map/ppermute | solution.py:267
  29.6 3.1 %lon_finish.1 = (f32[32,1152]{1,0:T(8,128)}, f32[1152,128]{1,0:T(8,128)}) custom-call(f32[1152,128]{1,0:T(8,128)} %get-tuple-element.19.partial, f32[1152,128]{1,0:T(8,128)} %get-tuple-element.20.decay, f32[16,1152]{1,0:T(8,128)} %get-tuple-element.22.own, f32[16,1152]{1,0:T(8,128)} %copy-done.6, f32[16,1152]{1,0:T(8,128)} %copy-done.4, ...), custom_call_target="tpu_custom_call" | custom-call | tf_op jit(solution)/shard_map/lon_finish/pallas_call | solution.py:247
  32.6 2.8 %collective-permute-start.8 = (f32[32,1152]{1,0:T(8,128)}, f32[32,1152]{1,0:T(8,128)S(1)}, u32[]{:S(2)}, u32[]{:S(2)}) collective-permute-start(f32[32,1152]{1,0:T(8,128)} %get-tuple-element.28.own), channel_id=1, source_target_pairs={{1,0},{2,1},{3,2},{0,3},{5,4},{6,5},{7,6},{4,7},{9,8},{10,9},{11,1... | collective-permute-start | bytes 442376 | tf_op jit(solution)/shard_map/ppermute | solution.py:267
  35.4 0.8 %collective-permute-start.7 = (f32[32,1152]{1,0:T(8,128)}, f32[32,1152]{1,0:T(8,128)S(1)}, u32[]{:S(2)}, u32[]{:S(2)}) collective-permute-start(f32[32,1152]{1,0:T(8,128)} %get-tuple-element.28.own), channel_id=1, source_target_pairs={{2,0},{3,1},{0,2},{1,3},{6,4},{7,5},{4,6},{5,7},{10,8},{11,9},{8,1... | collective-permute-start | bytes 442376 | tf_op jit(solution)/shard_map/ppermute | solution.py:267
  36.2 0.9 %collective-permute-start.6 = (f32[32,1152]{1,0:T(8,128)}, f32[32,1152]{1,0:T(8,128)S(1)}, u32[]{:S(2)}, u32[]{:S(2)}) collective-permute-start(f32[32,1152]{1,0:T(8,128)} %get-tuple-element.28.own), channel_id=1, source_target_pairs={{3,0},{0,1},{1,2},{2,3},{7,4},{4,5},{5,6},{6,7},{11,8},{8,9},{9,10... | collective-permute-start | bytes 442376 | tf_op jit(solution)/shard_map/ppermute | solution.py:267
  37.1 2.9 %collective-permute-done.8.third = f32[32,1152]{1,0:T(8,128)S(1)} collective-permute-done((f32[32,1152]{1,0:T(8,128)}, f32[32,1152]{1,0:T(8,128)S(1)}, u32[]{:S(2)}, u32[]{:S(2)}) %collective-permute-start.8) | collective-permute-done | bytes 147488 | tf_op jit(solution)/shard_map/ppermute | solution.py:267
  40.0 2.4 %collective-permute-done.7.second = f32[32,1152]{1,0:T(8,128)S(1)} collective-permute-done((f32[32,1152]{1,0:T(8,128)}, f32[32,1152]{1,0:T(8,128)S(1)}, u32[]{:S(2)}, u32[]{:S(2)}) %collective-permute-start.7) | collective-permute-done | bytes 147488 | tf_op jit(solution)/shard_map/ppermute | solution.py:267
  42.4 1.5 %collective-permute-done.6.first = f32[32,1152]{1,0:T(8,128)S(1)} collective-permute-done((f32[32,1152]{1,0:T(8,128)}, f32[32,1152]{1,0:T(8,128)S(1)}, u32[]{:S(2)}, u32[]{:S(2)}) %collective-permute-start.6) | collective-permute-done | bytes 147488 | tf_op jit(solution)/shard_map/ppermute | solution.py:267
  44.5 2.0 %lat_group.1 = (f32[32,1152]{1,0:T(8,128)}, f32[16,1152]{1,0:T(8,128)}, f32[16,1152]{1,0:T(8,128)}, f32[16,1152]{1,0:T(8,128)}) custom-call(f32[32,1152]{1,0:T(8,128)} %get-tuple-element.28.own, f32[32,1152]{1,0:T(8,128)} %copy-done.2, f32[32,1152]{1,0:T(8,128)} %copy-done.1, f32[32,1152]{1,0:T(8,128)} %copy-done, f32[8,1152]{1,0:T(8,128)} %constant.2.clone.table), custom_call_target="tpu_custom_call" | custom-call | tf_op jit(solution)/shard_map/lat_group/pallas_call | solution.py:247
  46.8 2.6 %collective-permute-start.10 = (f32[16,1152]{1,0:T(8,128)}, f32[16,1152]{1,0:T(8,128)S(1)}, u32[]{:S(2)}, u32[]{:S(2)}) collective-permute-start(f32[16,1152]{1,0:T(8,128)} %get-tuple-element.31), channel_id=1, source_target_pairs={{8,0},{9,1},{10,2},{11,3},{12,4},{13,5},{14,6},{15,7},{0,8},{1,9},... | collective-permute-start | bytes 221192 | tf_op jit(solution)/shard_map/ppermute | solution.py:267
  49.4 1.7 %collective-permute-done.9.first = f32[16,1152]{1,0:T(8,128)S(1)} collective-permute-done((f32[16,1152]{1,0:T(8,128)}, f32[16,1152]{1,0:T(8,128)S(1)}, u32[]{:S(2)}, u32[]{:S(2)}) %collective-permute-start.9) | collective-permute-done | bytes 73760 | tf_op jit(solution)/shard_map/ppermute | solution.py:267
  51.1 1.7 %collective-permute-done.10.second = f32[16,1152]{1,0:T(8,128)S(1)} collective-permute-done((f32[16,1152]{1,0:T(8,128)}, f32[16,1152]{1,0:T(8,128)S(1)}, u32[]{:S(2)}, u32[]{:S(2)}) %collective-permute-start.10) | collective-permute-done | bytes 73760 | tf_op jit(solution)/shard_map/ppermute | solution.py:267
  52.8 2.3 %collective-permute-done.11.third = f32[16,1152]{1,0:T(8,128)S(1)} collective-permute-done((f32[16,1152]{1,0:T(8,128)}, f32[16,1152]{1,0:T(8,128)S(1)}, u32[]{:S(2)}, u32[]{:S(2)}) %collective-permute-start.11) | collective-permute-done | bytes 73760 | tf_op jit(solution)/shard_map/ppermute | solution.py:267
  55.8 2.4 %lat_finish.1 = f32[128,1152]{1,0:T(8,128)} custom-call(f32[1152,128]{1,0:T(8,128)} %get-tuple-element.27.solved, f32[1152,128]{1,0:T(8,128)} %get-tuple-element.26.lat_decay.decay, f32[32,1152]{1,0:T(8,128)} %get-tuple-element.29.before, f32[16,1152]{1,0:T(8,128)} %copy-done.5, f32[16,1152]{1,0:T(8,128)} %copy-done.7, f32[16,1152]{1,0:T(8,128)} %copy-done.8, ...), custom_call_target="tpu_custom_call" | custom-call | tf_op jit(solution)/shard_map/lat_finish/pallas_call | solution.py:247
  (31 shorter events, 4.2 us)
Async XLA Ops:
  4.0 4.2 %collective-permute-start.2 = (f32[16,1152]{1,0:T(8,128)}, f32[16,1152]{1,0:T(8,128)S(1)}, u32[]{:S(2)}, u32[]{:S(2)}) collective-permute-start(f32[16,1152]{1,0:T(8,128)} %get-tuple-element.21.own), channel_id=1, source_target_pairs={{16,0},{32,16},{48,32},{0,48},{80,64},{96,80},{112,96},{64,112},{1... | collective-permute-start | bytes 221192 | tf_op jit(solution)/shard_map/ppermute | solution.py:267
  5.4 5.3 %collective-permute-start.1 = (f32[16,1152]{1,0:T(8,128)}, f32[16,1152]{1,0:T(8,128)S(1)}, u32[]{:S(2)}, u32[]{:S(2)}) collective-permute-start(f32[16,1152]{1,0:T(8,128)} %get-tuple-element.21.own), channel_id=1, source_target_pairs={{32,0},{48,16},{0,32},{16,48},{96,64},{112,80},{64,96},{80,112},{1... | collective-permute-start | bytes 221192 | tf_op jit(solution)/shard_map/ppermute | solution.py:267
  6.0 4.8 %collective-permute-start = (f32[16,1152]{1,0:T(8,128)}, f32[16,1152]{1,0:T(8,128)S(1)}, u32[]{:S(2)}, u32[]{:S(2)}) collective-permute-start(f32[16,1152]{1,0:T(8,128)} %get-tuple-element.21.own), channel_id=1, source_target_pairs={{48,0},{0,16},{16,32},{32,48},{112,64},{64,80},{80,96},{96,112},{1... | collective-permute-start | bytes 221192 | tf_op jit(solution)/shard_map/ppermute | solution.py:267
  8.3 2.5 %copy-start.9 = (f32[16,1152]{1,0:T(8,128)}, f32[16,1152]{1,0:T(8,128)S(1)}, u32[]{:S(2)}) copy-start(f32[16,1152]{1,0:T(8,128)S(1)} %collective-permute-done.2.third) | copy-start | bytes 221188
  10.7 0.6 %copy-start.10 = (f32[16,1152]{1,0:T(8,128)}, f32[16,1152]{1,0:T(8,128)S(1)}, u32[]{:S(2)}) copy-start(f32[16,1152]{1,0:T(8,128)S(1)} %collective-permute-done.1.second) | copy-start | bytes 221188
  11.4 0.6 %copy-start.11 = (f32[16,1152]{1,0:T(8,128)}, f32[16,1152]{1,0:T(8,128)S(1)}, u32[]{:S(2)}) copy-start(f32[16,1152]{1,0:T(8,128)S(1)} %collective-permute-done.first) | copy-start | bytes 221188
  13.7 13.0 %collective-permute-start.5 = (f32[16,1152]{1,0:T(8,128)}, f32[16,1152]{1,0:T(8,128)S(1)}, u32[]{:S(2)}, u32[]{:S(2)}) collective-permute-start(f32[16,1152]{1,0:T(8,128)} %get-tuple-element.22.own), channel_id=1, source_target_pairs={{64,0},{80,16},{96,32},{112,48},{128,64},{144,80},{160,96},{176,11... | collective-permute-start | bytes 221192 | tf_op jit(solution)/shard_map/ppermute | solution.py:267
  19.6 9.3 %collective-permute-start.4 = (f32[16,1152]{1,0:T(8,128)}, f32[16,1152]{1,0:T(8,128)S(1)}, u32[]{:S(2)}, u32[]{:S(2)}) collective-permute-start(f32[16,1152]{1,0:T(8,128)} %get-tuple-element.22.own), channel_id=1, source_target_pairs={{128,0},{144,16},{160,32},{176,48},{192,64},{208,80},{224,96},{240... | collective-permute-start | bytes 221192 | tf_op jit(solution)/shard_map/ppermute | solution.py:267
  20.6 8.4 %collective-permute-start.3 = (f32[16,1152]{1,0:T(8,128)}, f32[16,1152]{1,0:T(8,128)S(1)}, u32[]{:S(2)}, u32[]{:S(2)}) collective-permute-start(f32[16,1152]{1,0:T(8,128)} %get-tuple-element.22.own), channel_id=1, source_target_pairs={{192,0},{208,16},{224,32},{240,48},{0,64},{16,80},{32,96},{48,112}... | collective-permute-start | bytes 221192 | tf_op jit(solution)/shard_map/ppermute | solution.py:267
  26.7 2.2 %copy-start.3 = (f32[16,1152]{1,0:T(8,128)}, f32[16,1152]{1,0:T(8,128)S(1)}, u32[]{:S(2)}) copy-start(f32[16,1152]{1,0:T(8,128)S(1)} %collective-permute-done.5.third) | copy-start | bytes 221188
  28.9 0.6 %copy-start.4 = (f32[16,1152]{1,0:T(8,128)}, f32[16,1152]{1,0:T(8,128)S(1)}, u32[]{:S(2)}) copy-start(f32[16,1152]{1,0:T(8,128)S(1)} %collective-permute-done.4.second) | copy-start | bytes 221188
  28.9 0.7 %copy-start.6 = (f32[16,1152]{1,0:T(8,128)}, f32[16,1152]{1,0:T(8,128)S(1)}, u32[]{:S(2)}) copy-start(f32[16,1152]{1,0:T(8,128)S(1)} %collective-permute-done.3.first) | copy-start | bytes 221188
  32.6 7.3 %collective-permute-start.8 = (f32[32,1152]{1,0:T(8,128)}, f32[32,1152]{1,0:T(8,128)S(1)}, u32[]{:S(2)}, u32[]{:S(2)}) collective-permute-start(f32[32,1152]{1,0:T(8,128)} %get-tuple-element.28.own), channel_id=1, source_target_pairs={{1,0},{2,1},{3,2},{0,3},{5,4},{6,5},{7,6},{4,7},{9,8},{10,9},{11,1... | collective-permute-start | bytes 442376 | tf_op jit(solution)/shard_map/ppermute | solution.py:267
  35.4 7.0 %collective-permute-start.7 = (f32[32,1152]{1,0:T(8,128)}, f32[32,1152]{1,0:T(8,128)S(1)}, u32[]{:S(2)}, u32[]{:S(2)}) collective-permute-start(f32[32,1152]{1,0:T(8,128)} %get-tuple-element.28.own), channel_id=1, source_target_pairs={{2,0},{3,1},{0,2},{1,3},{6,4},{7,5},{4,6},{5,7},{10,8},{11,9},{8,1... | collective-permute-start | bytes 442376 | tf_op jit(solution)/shard_map/ppermute | solution.py:267
  36.2 7.6 %collective-permute-start.6 = (f32[32,1152]{1,0:T(8,128)}, f32[32,1152]{1,0:T(8,128)S(1)}, u32[]{:S(2)}, u32[]{:S(2)}) collective-permute-start(f32[32,1152]{1,0:T(8,128)} %get-tuple-element.28.own), channel_id=1, source_target_pairs={{3,0},{0,1},{1,2},{2,3},{7,4},{4,5},{5,6},{6,7},{11,8},{8,9},{9,10... | collective-permute-start | bytes 442376 | tf_op jit(solution)/shard_map/ppermute | solution.py:267
  40.0 3.8 %copy-start = (f32[32,1152]{1,0:T(8,128)}, f32[32,1152]{1,0:T(8,128)S(1)}, u32[]{:S(2)}) copy-start(f32[32,1152]{1,0:T(8,128)S(1)} %collective-permute-done.8.third) | copy-start | bytes 442372
  42.4 1.5 %copy-start.1 = (f32[32,1152]{1,0:T(8,128)}, f32[32,1152]{1,0:T(8,128)S(1)}, u32[]{:S(2)}) copy-start(f32[32,1152]{1,0:T(8,128)S(1)} %collective-permute-done.7.second) | copy-start | bytes 442372
  43.8 0.7 %copy-start.2 = (f32[32,1152]{1,0:T(8,128)}, f32[32,1152]{1,0:T(8,128)S(1)}, u32[]{:S(2)}) copy-start(f32[32,1152]{1,0:T(8,128)S(1)} %collective-permute-done.6.first) | copy-start | bytes 442372
  46.6 4.6 %collective-permute-start.9 = (f32[16,1152]{1,0:T(8,128)}, f32[16,1152]{1,0:T(8,128)S(1)}, u32[]{:S(2)}, u32[]{:S(2)}) collective-permute-start(f32[16,1152]{1,0:T(8,128)} %get-tuple-element.30), channel_id=1, source_target_pairs={{12,0},{13,1},{14,2},{15,3},{0,4},{1,5},{2,6},{3,7},{4,8},{5,9},{6... | collective-permute-start | bytes 221192 | tf_op jit(solution)/shard_map/ppermute | solution.py:267
  46.8 6.1 %collective-permute-start.10 = (f32[16,1152]{1,0:T(8,128)}, f32[16,1152]{1,0:T(8,128)S(1)}, u32[]{:S(2)}, u32[]{:S(2)}) collective-permute-start(f32[16,1152]{1,0:T(8,128)} %get-tuple-element.31), channel_id=1, source_target_pairs={{8,0},{9,1},{10,2},{11,3},{12,4},{13,5},{14,6},{15,7},{0,8},{1,9},... | collective-permute-start | bytes 221192 | tf_op jit(solution)/shard_map/ppermute | solution.py:267
  49.4 5.8 %collective-permute-start.11 = (f32[16,1152]{1,0:T(8,128)}, f32[16,1152]{1,0:T(8,128)S(1)}, u32[]{:S(2)}, u32[]{:S(2)}) collective-permute-start(f32[16,1152]{1,0:T(8,128)} %get-tuple-element.32), channel_id=1, source_target_pairs={{4,0},{5,1},{6,2},{7,3},{8,4},{9,5},{10,6},{11,7},{12,8},{13,9},{1... | collective-permute-start | bytes 221192 | tf_op jit(solution)/shard_map/ppermute | solution.py:267
  51.1 4.0 %copy-start.5 = (f32[16,1152]{1,0:T(8,128)}, f32[16,1152]{1,0:T(8,128)S(1)}, u32[]{:S(2)}) copy-start(f32[16,1152]{1,0:T(8,128)S(1)} %collective-permute-done.9.first) | copy-start | bytes 221188
  52.8 2.3 %copy-start.7 = (f32[16,1152]{1,0:T(8,128)}, f32[16,1152]{1,0:T(8,128)S(1)}, u32[]{:S(2)}) copy-start(f32[16,1152]{1,0:T(8,128)S(1)} %collective-permute-done.10.second) | copy-start | bytes 221188
  55.1 0.6 %copy-start.8 = (f32[16,1152]{1,0:T(8,128)}, f32[16,1152]{1,0:T(8,128)S(1)}, u32[]{:S(2)}) copy-start(f32[16,1152]{1,0:T(8,128)S(1)} %collective-permute-done.11.third) | copy-start | bytes 221188

commit v2 on v1

--- a/solution.py
+++ b/solution.py
@@ -43,11 +43,33 @@
     return second[0] * first[0], second[0] * first[1] + second[1]
 
 
-def lon_local(wave, speed, mask, table, message, partial, decay):
-    count, lats = mask.shape
+def lon_local(
+    wave_far, speed_far, mask_far, table_far, message, partial, decay,
+    wave, speed, mask, table, arrived,
+):
+    lats, count = mask.shape
     rows = count * lats
-    sea = mask[...].astype(jnp.float32).T
-    for part in chunks(wave.shape[1]):
+    parts = chunks(wave.shape[1])
+    small = [
+        pltpu.make_async_copy(mask_far, mask, arrived.at[0]),
+        pltpu.make_async_copy(table_far, table, arrived.at[1]),
+    ]
+    large = [
+        [
+            pltpu.make_async_copy(far.at[:, part], near.at[:, part], arrived.at[2 * n + which])
+            for which, (far, near) in enumerate(((wave_far, wave), (speed_far, speed)))
+        ]
+        for n, part in enumerate(parts, 1)
+    ]
+    for copies in (small, *large):
+        for copy in copies:
+            copy.start()
+    for copy in small:
+        copy.wait()
+    sea = mask[...].astype(jnp.float32)
+    for part, copies in zip(parts, large):
+        for copy in copies:
+            copy.wait()
         cosine, east = table[0:1, part], table[2:3, part] > 0.5
 
         def row(i):
@@ -76,28 +98,16 @@
         message[lats : 2 * lats, part] = value
 
 
-def lat_coefficients(speed, mask, edges, table, ratio, scaled, decay, rate, arrived):
-    lons, count = mask.shape
+def lat_coefficients(speed, mask, edges, table, ratio, scaled, decay, rate):
+    count, lons = mask.shape
     rows = lons * count
-    parts = chunks(speed.shape[1])
-
-    def copy(tile):
-        lanes = pl.ds(tile * LANES, LANES)
-        return pltpu.make_async_copy(
-            speed.at[:, lanes], rate.at[pl.ds(tile * rows, rows), :], arrived.at[tile]
-        )
-
-    for part in parts:
-        for tile in tiles_of(part):
-            copy(tile).start()
     place, last = lax.axis_index("lat"), lax.axis_size("lat") - 1
-    sea = mask[...].astype(jnp.float32)
+    sea = mask[...].astype(jnp.float32).T
     opened = edges[...].astype(jnp.float32).T
     south = jnp.where(place == 0, opened[:, 0:1], 1.0)
     north = jnp.where(place == last, opened[:, 1:2], 1.0)
-    for part in parts:
-        for tile in tiles_of(part):
-            copy(tile).wait()
+    for part in chunks(speed.shape[1]):
+        put(rate, rows, part, 0, speed[:, part])
         sine, up = table[1:2, part], table[3:4, part] > 0.5
         flows = [
             take(rate, rows, part, j, lons, count) * sine * sea[:, j : j + 1] for j in range(count)
@@ -243,13 +253,18 @@
 
 
 def run(kernel, shapes, *operands, scratch=(), far_inputs=(), far_outputs=()):
-    here, away = pl.BlockSpec(memory_space=pltpu.VMEM), pl.BlockSpec(memory_space=pl.ANY)
+    here, away = pl.BlockSpec(memory_space=pltpu.VMEM), pl.BlockSpec(memory_space=pltpu.HBM)
+    operands = [
+        pltpu.with_memory_space_constraint(x, pltpu.HBM) if n in far_inputs else x
+        for n, x in enumerate(operands)
+    ]
     return pl.pallas_call(
         kernel,
         out_shape=[jax.ShapeDtypeStruct(shape, jnp.float32) for shape in shapes],
         in_specs=[away if n in far_inputs else here for n in range(len(operands))],
         out_specs=[away if n in far_outputs else here for n in range(len(shapes))],
         scratch_shapes=scratch,
+        compiler_params=pltpu.CompilerParams(vmem_limit_bytes=8 << 20),
         name=kernel.__name__,
     )(*operands)
 
@@ -278,11 +293,19 @@
     buffer = pltpu.VMEM(tiled, jnp.float32)
     signals = pltpu.SemaphoreType.DMA((bins // LANES,))
 
-    own, partial, decay = run(lon_local, [small, tiled, tiled], wave, speed, land_mask, table)
+    sea = land_mask.T
+    own, partial, decay = run(
+        lon_local, [small, tiled, tiled], wave, speed, sea, table,
+        scratch=[
+            pltpu.VMEM(flat, jnp.float32), pltpu.VMEM(flat, jnp.float32),
+            pltpu.VMEM(sea.shape, sea.dtype), pltpu.VMEM(table.shape, table.dtype),
+            pltpu.SemaphoreType.DMA((2 + 2 * len(chunks(bins)),)),
+        ],
+        far_inputs=range(4),
+    )
     near = exchange(own, "lon", True)
     ratio, scaled, lat_decay = run(
-        lat_coefficients, [tiled] * 3, lat_rate, land_mask, open_edges, table,
-        scratch=[buffer, signals], far_inputs=(0,),
+        lat_coefficients, [tiled] * 3, lat_rate, sea, open_edges, table, scratch=[buffer]
     )
     whole, before = run(lon_group, [small, small], own, *near, table)
     far = exchange(whole, "lon", False)

time: 58.5 us -> 44.9 us (0.77)
  Pallas kernels: 15.2 us -> 3.6 us
  local copies, waits for them, and re-layouts: 4.54 us -> 0.02 us
  waiting for transfers between devices: 19.3 us -> 21.6 us
    pallas_call x6, Pallas kernels: 15.2 us -> 3.6 us  [run(): pl.pallas_call(kernel, out_shape=[jax.ShapeDtypeStruct(shape, jnp.float32...]
    unnamed x25 -> x8, local copies, waits for them, and re-layouts: 4.54 us -> 0.02 us
    ppermute x12, waiting for transfers between devices: 19.3 us -> 21.6 us  [exchange(): lax.ppermute(item, axis, route(d))]
  transfers between devices with their start and end apart: 12 -> 12, of which waited for: 9 -> 11; matrix products, arithmetic and copies ran while one was open for 0% -> 0% of each run, Pallas kernels for 6% -> 1%
where the time goes in v2:
time: 44.9 us; the launch traced here: 44.8 us
  waiting for transfers between devices  21.6 us (48%)
  starting transfers between devices  19.5 us (43%)
  Pallas kernels  3.6 us (8%)
    ppermute x12, waiting for transfers between devices, exchange(): lax.ppermute(item, axis, route(d))  21.6 us
    ppermute x12, starting transfers between devices, exchange(): lax.ppermute(item, axis, route(d))  19.5 us
    pallas_call x6, Pallas kernels, run(): pl.pallas_call(kernel, out_shape=[jax.ShapeDtypeStruct(shape, jnp.float32...  3.6 us
  transfers between devices with their start and end apart: 12, of which 11 were waited for; matrix products, arithmetic and copies ran while one was open for 0% of the time, Pallas kernels for 1%

profile of v2, /device:TPU:24, one launch (start us, length us, event | category | flops | bytes accessed | tf_op | source)
XLA Modules:
  0.0 44.8 jit_solution(6039898456164712036)
XLA Ops:
  0.0 1.6 %lon_local.1 = (f32[16,1152]{1,0:T(8,128)S(1)}, f32[1152,128]{1,0:T(8,128)S(1)}, f32[1152,128]{1,0:T(8,128)S(1)}) custom-call(f32[128,1152]{1,0:T(8,128)} %bitcast.8, f32[128,1152]{1,0:T(8,128)} %bitcast.9, s32[8,16]{1,0:T(8,128)} %bitcast.6, f32[8,1152]{1,0:T(8,128)} %constant.2.clone.table_far.table), custom_call_target="tpu_custom_call" | custom-call | tf_op jit(solution)/shard_map/lon_local/pallas_call | solution.py:261
  1.6 1.4 %collective-permute-start.2 = (f32[16,1152]{1,0:T(8,128)S(1)}, f32[16,1152]{1,0:T(8,128)S(1)}, u32[]{:S(2)}, u32[]{:S(2)}) collective-permute-start(f32[16,1152]{1,0:T(8,128)S(1)} %get-tuple-element.21.own), channel_id=1, source_target_pairs={{16,0},{32,16},{48,32},{0,48},{80,64},{96,80},{112,96},{64,112},{1... | collective-permute-start | bytes 221192 | tf_op jit(solution)/shard_map/ppermute | solution.py:282
  3.0 0.7 %collective-permute-start.1 = (f32[16,1152]{1,0:T(8,128)S(1)}, f32[16,1152]{1,0:T(8,128)S(1)}, u32[]{:S(2)}, u32[]{:S(2)}) collective-permute-start(f32[16,1152]{1,0:T(8,128)S(1)} %get-tuple-element.21.own), channel_id=1, source_target_pairs={{32,0},{48,16},{0,32},{16,48},{96,64},{112,80},{64,96},{80,112},{1... | collective-permute-start | bytes 221192 | tf_op jit(solution)/shard_map/ppermute | solution.py:282
  3.8 1.8 %collective-permute-done.2.third = f32[16,1152]{1,0:T(8,128)S(1)} collective-permute-done((f32[16,1152]{1,0:T(8,128)S(1)}, f32[16,1152]{1,0:T(8,128)S(1)}, u32[]{:S(2)}, u32[]{:S(2)}) %collective-permute-start.2) | collective-permute-done | bytes 73760 | tf_op jit(solution)/shard_map/ppermute | solution.py:282
  5.6 2.5 %collective-permute-done.1.second = f32[16,1152]{1,0:T(8,128)S(1)} collective-permute-done((f32[16,1152]{1,0:T(8,128)S(1)}, f32[16,1152]{1,0:T(8,128)S(1)}, u32[]{:S(2)}, u32[]{:S(2)}) %collective-permute-start.1) | collective-permute-done | bytes 73760 | tf_op jit(solution)/shard_map/ppermute | solution.py:282
  8.3 6.0 %collective-permute-start.5 = (f32[16,1152]{1,0:T(8,128)S(1)}, f32[16,1152]{1,0:T(8,128)S(1)}, u32[]{:S(2)}, u32[]{:S(2)}) collective-permute-start(f32[16,1152]{1,0:T(8,128)S(1)} %get-tuple-element.22.own), channel_id=1, source_target_pairs={{64,0},{80,16},{96,32},{112,48},{128,64},{144,80},{160,96},{176,11... | collective-permute-start | bytes 221192 | tf_op jit(solution)/shard_map/ppermute | solution.py:282
  14.3 1.0 %collective-permute-start.4 = (f32[16,1152]{1,0:T(8,128)S(1)}, f32[16,1152]{1,0:T(8,128)S(1)}, u32[]{:S(2)}, u32[]{:S(2)}) collective-permute-start(f32[16,1152]{1,0:T(8,128)S(1)} %get-tuple-element.22.own), channel_id=1, source_target_pairs={{128,0},{144,16},{160,32},{176,48},{192,64},{208,80},{224,96},{240... | collective-permute-start | bytes 221192 | tf_op jit(solution)/shard_map/ppermute | solution.py:282
  15.3 2.8 %collective-permute-start.3 = (f32[16,1152]{1,0:T(8,128)S(1)}, f32[16,1152]{1,0:T(8,128)S(1)}, u32[]{:S(2)}, u32[]{:S(2)}) collective-permute-start(f32[16,1152]{1,0:T(8,128)S(1)} %get-tuple-element.22.own), channel_id=1, source_target_pairs={{192,0},{208,16},{224,32},{240,48},{0,64},{16,80},{32,96},{48,112}... | collective-permute-start | bytes 221192 | tf_op jit(solution)/shard_map/ppermute | solution.py:282
  18.2 0.3 lat_coefficients.1
  18.5 0.3 collective-permute-done.5.third
  18.8 4.9 %collective-permute-done.4.second = f32[16,1152]{1,0:T(8,128)S(1)} collective-permute-done((f32[16,1152]{1,0:T(8,128)S(1)}, f32[16,1152]{1,0:T(8,128)S(1)}, u32[]{:S(2)}, u32[]{:S(2)}) %collective-permute-start.4) | collective-permute-done | bytes 73760 | tf_op jit(solution)/shard_map/ppermute | solution.py:282
  23.7 0.3 lon_finish.1
  24.0 2.8 %collective-permute-start.8 = (f32[32,1152]{1,0:T(8,128)S(1)}, f32[32,1152]{1,0:T(8,128)S(1)}, u32[]{:S(2)}, u32[]{:S(2)}) collective-permute-start(f32[32,1152]{1,0:T(8,128)S(1)} %get-tuple-element.28.own), channel_id=1, source_target_pairs={{1,0},{2,1},{3,2},{0,3},{5,4},{6,5},{7,6},{4,7},{9,8},{10,9},{11,1... | collective-permute-start | bytes 442376 | tf_op jit(solution)/shard_map/ppermute | solution.py:282
  26.8 0.8 %collective-permute-start.7 = (f32[32,1152]{1,0:T(8,128)S(1)}, f32[32,1152]{1,0:T(8,128)S(1)}, u32[]{:S(2)}, u32[]{:S(2)}) collective-permute-start(f32[32,1152]{1,0:T(8,128)S(1)} %get-tuple-element.28.own), channel_id=1, source_target_pairs={{2,0},{3,1},{0,2},{1,3},{6,4},{7,5},{4,6},{5,7},{10,8},{11,9},{8,1... | collective-permute-start | bytes 442376 | tf_op jit(solution)/shard_map/ppermute | solution.py:282
  27.6 0.9 %collective-permute-start.6 = (f32[32,1152]{1,0:T(8,128)S(1)}, f32[32,1152]{1,0:T(8,128)S(1)}, u32[]{:S(2)}, u32[]{:S(2)}) collective-permute-start(f32[32,1152]{1,0:T(8,128)S(1)} %get-tuple-element.28.own), channel_id=1, source_target_pairs={{3,0},{0,1},{1,2},{2,3},{7,4},{4,5},{5,6},{6,7},{11,8},{8,9},{9,10... | collective-permute-start | bytes 442376 | tf_op jit(solution)/shard_map/ppermute | solution.py:282
  28.5 2.6 %collective-permute-done.8.third = f32[32,1152]{1,0:T(8,128)S(1)} collective-permute-done((f32[32,1152]{1,0:T(8,128)S(1)}, f32[32,1152]{1,0:T(8,128)S(1)}, u32[]{:S(2)}, u32[]{:S(2)}) %collective-permute-start.8) | collective-permute-done | bytes 147488 | tf_op jit(solution)/shard_map/ppermute | solution.py:282
  31.1 2.5 %collective-permute-done.7.second = f32[32,1152]{1,0:T(8,128)S(1)} collective-permute-done((f32[32,1152]{1,0:T(8,128)S(1)}, f32[32,1152]{1,0:T(8,128)S(1)}, u32[]{:S(2)}, u32[]{:S(2)}) %collective-permute-start.7) | collective-permute-done | bytes 147488 | tf_op jit(solution)/shard_map/ppermute | solution.py:282
  33.6 1.5 %collective-permute-done.6.first = f32[32,1152]{1,0:T(8,128)S(1)} collective-permute-done((f32[32,1152]{1,0:T(8,128)S(1)}, f32[32,1152]{1,0:T(8,128)S(1)}, u32[]{:S(2)}, u32[]{:S(2)}) %collective-permute-start.6) | collective-permute-done | bytes 147488 | tf_op jit(solution)/shard_map/ppermute | solution.py:282
  35.3 0.3 collective-permute-start.9
  35.6 2.6 %collective-permute-start.10 = (f32[16,1152]{1,0:T(8,128)S(1)}, f32[16,1152]{1,0:T(8,128)S(1)}, u32[]{:S(2)}, u32[]{:S(2)}) collective-permute-start(f32[16,1152]{1,0:T(8,128)S(1)} %get-tuple-element.31), channel_id=1, source_target_pairs={{8,0},{9,1},{10,2},{11,3},{12,4},{13,5},{14,6},{15,7},{0,8},{1,9},... | collective-permute-start | bytes 221192 | tf_op jit(solution)/shard_map/ppermute | solution.py:282
  38.2 1.5 %collective-permute-done.9.first = f32[16,1152]{1,0:T(8,128)S(1)} collective-permute-done((f32[16,1152]{1,0:T(8,128)S(1)}, f32[16,1152]{1,0:T(8,128)S(1)}, u32[]{:S(2)}, u32[]{:S(2)}) %collective-permute-start.9) | collective-permute-done | bytes 73760 | tf_op jit(solution)/shard_map/ppermute | solution.py:282
  39.7 1.7 %collective-permute-done.10.second = f32[16,1152]{1,0:T(8,128)S(1)} collective-permute-done((f32[16,1152]{1,0:T(8,128)S(1)}, f32[16,1152]{1,0:T(8,128)S(1)}, u32[]{:S(2)}, u32[]{:S(2)}) %collective-permute-start.10) | collective-permute-done | bytes 73760 | tf_op jit(solution)/shard_map/ppermute | solution.py:282
  41.4 2.3 %collective-permute-done.11.third = f32[16,1152]{1,0:T(8,128)S(1)} collective-permute-done((f32[16,1152]{1,0:T(8,128)S(1)}, f32[16,1152]{1,0:T(8,128)S(1)}, u32[]{:S(2)}, u32[]{:S(2)}) %collective-permute-start.11) | collective-permute-done | bytes 73760 | tf_op jit(solution)/shard_map/ppermute | solution.py:282
  43.7 1.0 %lat_finish.1 = f32[128,1152]{1,0:T(8,128)} custom-call(f32[1152,128]{1,0:T(8,128)S(1)} %get-tuple-element.27.solved, f32[1152,128]{1,0:T(8,128)S(1)} %get-tuple-element.26.lat_decay.decay, f32[32,1152]{1,0:T(8,128)S(1)} %get-tuple-element.29.before, f32[16,1152]{1,0:T(8,128)S(1)} %collective-permute-done.9.first, ...), custom_call_target="tpu_custom_call" | custom-call | tf_op jit(solution)/shard_map/lat_finish/pallas_call | solution.py:261
  (14 shorter events, 0.6 us)
Async XLA Ops:
  0.0 8.2 %copy-start = (f32[8,1152]{1,0:T(8,128)S(1)}, f32[8,1152]{1,0:T(8,128)}, u32[]{:S(2)}) copy-start(f32[8,1152]{1,0:T(8,128)} %constant.2.clone.table_far.table) | copy-start | bytes 110596
  0.0 18.2 %copy-start.1 = (f32[16,8,1152]{2,1,0:T(8,128)S(1)}, f32[16,8,1152]{2,1,0:T(8,128)}, u32[]{:S(2)}) copy-start(f32[16,8,1152]{2,1,0:T(8,128)} %param.8) | copy-start | bytes 1769476
  1.6 4.0 %collective-permute-start.2 = (f32[16,1152]{1,0:T(8,128)S(1)}, f32[16,1152]{1,0:T(8,128)S(1)}, u32[]{:S(2)}, u32[]{:S(2)}) collective-permute-start(f32[16,1152]{1,0:T(8,128)S(1)} %get-tuple-element.21.own), channel_id=1, source_target_pairs={{16,0},{32,16},{48,32},{0,48},{80,64},{96,80},{112,96},{64,112},{1... | collective-permute-start | bytes 221192 | tf_op jit(solution)/shard_map/ppermute | solution.py:282
  3.0 5.1 %collective-permute-start.1 = (f32[16,1152]{1,0:T(8,128)S(1)}, f32[16,1152]{1,0:T(8,128)S(1)}, u32[]{:S(2)}, u32[]{:S(2)}) collective-permute-start(f32[16,1152]{1,0:T(8,128)S(1)} %get-tuple-element.21.own), channel_id=1, source_target_pairs={{32,0},{48,16},{0,32},{16,48},{96,64},{112,80},{64,96},{80,112},{1... | collective-permute-start | bytes 221192 | tf_op jit(solution)/shard_map/ppermute | solution.py:282
  3.7 4.5 %collective-permute-start = (f32[16,1152]{1,0:T(8,128)S(1)}, f32[16,1152]{1,0:T(8,128)S(1)}, u32[]{:S(2)}, u32[]{:S(2)}) collective-permute-start(f32[16,1152]{1,0:T(8,128)S(1)} %get-tuple-element.21.own), channel_id=1, source_target_pairs={{48,0},{0,16},{16,32},{32,48},{112,64},{64,80},{80,96},{96,112},{1... | collective-permute-start | bytes 221192 | tf_op jit(solution)/shard_map/ppermute | solution.py:282
  8.2 10.0 %copy-start.2 = (s32[16,8]{0,1:T(8,128)S(1)}, s32[16,8]{0,1:T(8,128)}, u32[]{:S(2)}) copy-start(s32[16,8]{0,1:T(8,128)} %param.9) | copy-start | bytes 1540
  8.3 9.9 %copy-start.3 = (s32[2,16]{1,0:T(2,128)S(1)}, s32[2,16]{1,0:T(2,128)}, u32[]{:S(2)}) copy-start(s32[2,16]{1,0:T(2,128)} %edges.1) | copy-start | bytes 388
  8.3 10.5 %collective-permute-start.5 = (f32[16,1152]{1,0:T(8,128)S(1)}, f32[16,1152]{1,0:T(8,128)S(1)}, u32[]{:S(2)}, u32[]{:S(2)}) collective-permute-start(f32[16,1152]{1,0:T(8,128)S(1)} %get-tuple-element.22.own), channel_id=1, source_target_pairs={{64,0},{80,16},{96,32},{112,48},{128,64},{144,80},{160,96},{176,11... | collective-permute-start | bytes 221192 | tf_op jit(solution)/shard_map/ppermute | solution.py:282
  14.3 9.3 %collective-permute-start.4 = (f32[16,1152]{1,0:T(8,128)S(1)}, f32[16,1152]{1,0:T(8,128)S(1)}, u32[]{:S(2)}, u32[]{:S(2)}) collective-permute-start(f32[16,1152]{1,0:T(8,128)S(1)} %get-tuple-element.22.own), channel_id=1, source_target_pairs={{128,0},{144,16},{160,32},{176,48},{192,64},{208,80},{224,96},{240... | collective-permute-start | bytes 221192 | tf_op jit(solution)/shard_map/ppermute | solution.py:282
  15.3 8.3 %collective-permute-start.3 = (f32[16,1152]{1,0:T(8,128)S(1)}, f32[16,1152]{1,0:T(8,128)S(1)}, u32[]{:S(2)}, u32[]{:S(2)}) collective-permute-start(f32[16,1152]{1,0:T(8,128)S(1)} %get-tuple-element.22.own), channel_id=1, source_target_pairs={{192,0},{208,16},{224,32},{240,48},{0,64},{16,80},{32,96},{48,112}... | collective-permute-start | bytes 221192 | tf_op jit(solution)/shard_map/ppermute | solution.py:282
  24.0 7.1 %collective-permute-start.8 = (f32[32,1152]{1,0:T(8,128)S(1)}, f32[32,1152]{1,0:T(8,128)S(1)}, u32[]{:S(2)}, u32[]{:S(2)}) collective-permute-start(f32[32,1152]{1,0:T(8,128)S(1)} %get-tuple-element.28.own), channel_id=1, source_target_pairs={{1,0},{2,1},{3,2},{0,3},{5,4},{6,5},{7,6},{4,7},{9,8},{10,9},{11,1... | collective-permute-start | bytes 442376 | tf_op jit(solution)/shard_map/ppermute | solution.py:282
  26.8 6.7 %collective-permute-start.7 = (f32[32,1152]{1,0:T(8,128)S(1)}, f32[32,1152]{1,0:T(8,128)S(1)}, u32[]{:S(2)}, u32[]{:S(2)}) collective-permute-start(f32[32,1152]{1,0:T(8,128)S(1)} %get-tuple-element.28.own), channel_id=1, source_target_pairs={{2,0},{3,1},{0,2},{1,3},{6,4},{7,5},{4,6},{5,7},{10,8},{11,9},{8,1... | collective-permute-start | bytes 442376 | tf_op jit(solution)/shard_map/ppermute | solution.py:282
  27.6 7.4 %collective-permute-start.6 = (f32[32,1152]{1,0:T(8,128)S(1)}, f32[32,1152]{1,0:T(8,128)S(1)}, u32[]{:S(2)}, u32[]{:S(2)}) collective-permute-start(f32[32,1152]{1,0:T(8,128)S(1)} %get-tuple-element.28.own), channel_id=1, source_target_pairs={{3,0},{0,1},{1,2},{2,3},{7,4},{4,5},{5,6},{6,7},{11,8},{8,9},{9,10... | collective-permute-start | bytes 442376 | tf_op jit(solution)/shard_map/ppermute | solution.py:282
  35.3 4.4 %collective-permute-start.9 = (f32[16,1152]{1,0:T(8,128)S(1)}, f32[16,1152]{1,0:T(8,128)S(1)}, u32[]{:S(2)}, u32[]{:S(2)}) collective-permute-start(f32[16,1152]{1,0:T(8,128)S(1)} %get-tuple-element.30), channel_id=1, source_target_pairs={{12,0},{13,1},{14,2},{15,3},{0,4},{1,5},{2,6},{3,7},{4,8},{5,9},{6... | collective-permute-start | bytes 221192 | tf_op jit(solution)/shard_map/ppermute | solution.py:282
  35.6 5.9 %collective-permute-start.10 = (f32[16,1152]{1,0:T(8,128)S(1)}, f32[16,1152]{1,0:T(8,128)S(1)}, u32[]{:S(2)}, u32[]{:S(2)}) collective-permute-start(f32[16,1152]{1,0:T(8,128)S(1)} %get-tuple-element.31), channel_id=1, source_target_pairs={{8,0},{9,1},{10,2},{11,3},{12,4},{13,5},{14,6},{15,7},{0,8},{1,9},... | collective-permute-start | bytes 221192 | tf_op jit(solution)/shard_map/ppermute | solution.py:282
  38.2 5.6 %collective-permute-start.11 = (f32[16,1152]{1,0:T(8,128)S(1)}, f32[16,1152]{1,0:T(8,128)S(1)}, u32[]{:S(2)}, u32[]{:S(2)}) collective-permute-start(f32[16,1152]{1,0:T(8,128)S(1)} %get-tuple-element.32), channel_id=1, source_target_pairs={{4,0},{5,1},{6,2},{7,3},{8,4},{9,5},{10,6},{11,7},{12,8},{13,9},{1... | collective-permute-start | bytes 221192 | tf_op jit(solution)/shard_map/ppermute | solution.py:282

commit v3 on v2

--- a/solution.py
+++ b/solution.py
@@ -44,7 +44,7 @@
 
 
 def lon_local(
-    wave_far, speed_far, mask_far, table_far, message, partial, decay,
+    wave_far, speed_far, mask_far, table_far, keep, give, partial, decay,
     wave, speed, mask, table, arrived,
 ):
     lats, count = mask.shape
@@ -67,6 +67,7 @@
     for copy in small:
         copy.wait()
     sea = mask[...].astype(jnp.float32)
+    first_core = lax.axis_index("lon") % 2 == 0
     for part, copies in zip(parts, large):
         for copy in copies:
             copy.wait()
@@ -94,11 +95,15 @@
             total = a if k == 0 else a * total
             put(partial, rows, part, k * lats, value)
             put(decay, rows, part, k * lats, total)
-        message[0:lats, part] = total
-        message[lats : 2 * lats, part] = value
-
-
-def lat_coefficients(speed, mask, edges, table, ratio, scaled, decay, rate):
+        low, high = (
+            jnp.concatenate([state[rows] for state in (total, value)], axis=0)
+            for rows in (slice(0, lats // 2), slice(lats // 2, lats))
+        )
+        keep[:, part] = jnp.where(first_core, low, high)
+        give[:, part] = jnp.where(first_core, high, low)
+
+
+def lat_coefficients(speed, mask, edges, table, ratio, scaled, decay, whole, rate):
     count, lons = mask.shape
     rows = lons * count
     place, last = lax.axis_index("lat"), lax.axis_size("lat") - 1
@@ -122,15 +127,16 @@
             put(ratio, rows, part, k * lons, a)
             put(scaled, rows, part, k * lons, scale)
             put(decay, rows, part, k * lons, total)
-
-
-def ordered_group(own, received, place, positive):
+        whole[:, part] = total
+
+
+def ordered_group(own, received, place, positive, wanted=()):
     members = [own, *received]
     in_place = []
     for slot in range(4):
         value = members[0]
         for d in range(1, 4):
-            hit = (place + 4 - slot) % 4 == d
+            hit = place ^ slot == d
             value = [jnp.where(hit, new, old) for new, old in zip(members[d], value)]
         in_place.append(value)
     swept = [
@@ -148,8 +154,10 @@
             value = [jnp.where(index == slot, new, old) for new, old in zip(prefixes[slot], value)]
         return value
 
-    before = [jnp.where(positive, low, high) for low, high in zip(chosen(place), chosen(3 - place))]
-    return whole, before
+    return whole, *(
+        [jnp.where(positive, low, high) for low, high in zip(chosen(at), chosen(3 - at))]
+        for at in wanted or (place,)
+    )
 
 
 def halves(ref, part):
@@ -157,32 +165,44 @@
     return [ref[0:rows, part], ref[rows : 2 * rows, part]]
 
 
-def lon_group(own, first, second, third, table, whole, before):
+def store(ref, part, state):
+    rows = ref.shape[0] // 2
+    ref[0:rows, part], ref[rows : 2 * rows, part] = state
+
+
+def lon_group(own, first, second, third, table, whole, before, before_partner):
     place = lax.axis_index("lon") % 4
-    rows = own.shape[0] // 2
     for part in chunks(own.shape[1]):
         received = [halves(ref, part) for ref in (first, second, third)]
-        total, prefix = ordered_group(halves(own, part), received, place, table[2:3, part] > 0.5)
-        whole[0:rows, part], whole[rows : 2 * rows, part] = total
-        before[0:rows, part], before[rows : 2 * rows, part] = prefix
-
-
-def lon_finish(
-    partial, decay, own, first, second, third, before, ratio, scaled, lat_decay, table,
-    message, solved, half,
-):
-    lats, lons = own.shape[0] // 2, message.shape[0] // 2
+        states = ordered_group(
+            halves(own, part), received, place, table[2:3, part] > 0.5, (place, place ^ 1)
+        )
+        for ref, state in zip((whole, before, before_partner), states):
+            store(ref, part, state)
+
+
+def lon_cycle(own, first, second, third, before, before_partner, table, keep, give):
+    place = lax.axis_index("lon") // 4
+    for part in chunks(own.shape[1]):
+        received = [halves(ref, part) for ref in (first, second, third)]
+        cycle, start = ordered_group(halves(own, part), received, place, table[2:3, part] > 0.5)
+        entering = cycle[1] / (1.0 - cycle[0])
+        entering = start[0] * entering + start[1]
+        for ref, state in ((keep, before), (give, before_partner)):
+            a, b = halves(state, part)
+            ref[:, part] = a * entering + b
+
+
+def lon_finish(partial, decay, kept, given, ratio, scaled, table, message, solved, half):
+    lats, lons = 2 * kept.shape[0], message.shape[0]
     rows = lons * lats
-    for part in chunks(own.shape[1]):
+    first_core = lax.axis_index("lon") % 2 == 0
+    for part in chunks(kept.shape[1]):
         east, up = table[2:3, part] > 0.5, table[3:4, part] > 0.5
-        one, two, three = (halves(ref, part) for ref in (first, second, third))
-        cycle = halves(own, part)
-        cycle = compose(cycle, [jnp.where(east, x, y) for x, y in zip(three, one)])
-        cycle = compose(cycle, two)
-        cycle = compose(cycle, [jnp.where(east, x, y) for x, y in zip(one, three)])
-        entering = cycle[1] / (1.0 - cycle[0])
-        prefix = halves(before, part)
-        entering = prefix[0] * entering + prefix[1]
+        mine, other = kept[:, part], given[:, part]
+        entering = jnp.concatenate(
+            [jnp.where(first_core, mine, other), jnp.where(first_core, other, mine)], axis=0
+        )
         for k in range(lons // 2):
             low, high = k * lats, (lons - 1 - k) * lats
             a, b = (
@@ -198,35 +218,65 @@
             step = step * jnp.where(up, lines[k], lines[lats - 1 - k])
             value = step if k == 0 else take(ratio, rows, part, k * lons, lons) * value + step
             put(solved, rows, part, k * lons, value)
-        message[0:lons, part] = take(lat_decay, rows, part, (lats - 1) * lons, lons)
-        message[lons : 2 * lons, part] = value
-
-
-def lat_group(own, first, second, third, table, before, *messages):
+        message[:, part] = value
+
+
+def packed(value, positive):
+    rows = value.shape[0] // 2
+    low, high = value[0:rows], pltpu.roll(value[rows : 2 * rows], HALF, 1)
+    return jnp.where(positive, low, high), jnp.where(positive, high, low)
+
+
+def unpacked(message):
+    bins = message.shape[1]
+    return jnp.concatenate([message, pltpu.roll(message, bins - HALF, 1)], axis=0)
+
+
+def lat_group_ahead(own, first, second, third, table, *messages):
+    row = lax.axis_index("lat") // 4
+    total = own[...] * first[...] * second[...] * third[...]
+    north, south = packed(total, table[3:4, :] > 0.5)
+    for d, message in enumerate(messages, 1):
+        message[...] = jnp.where(row ^ d > row, north, south)
+
+
+def lat_group(own, own_ahead, first, second, third, *rest):
+    *ahead, table, before, message_1, message_2, message_3 = rest
     place = lax.axis_index("lat")
-    rows = own.shape[0] // 2
-    everything = slice(0, own.shape[1])
-    received = [halves(ref, everything) for ref in (first, second, third)]
+    row = place // 4
+    rows = own.shape[0]
+    received = [[a[...], b[...]] for a, b in zip(ahead, (first, second, third))]
     up = table[3:4, :] > 0.5
-    total, prefix = ordered_group(halves(own, everything), received, place % 4, up)
+    total, prefix = ordered_group([own_ahead[...], own[...]], received, place % 4, up)
     before[0:rows], before[rows : 2 * rows] = prefix
-    turned = pltpu.roll(total[1], HALF, 1)
-    north, south = jnp.where(up, total[0], turned), jnp.where(up, turned, total[0])
-    for d, message in enumerate(messages, 1):
-        message[...] = jnp.where(place // 4 + d < 4, north, south)
-
-
-def lat_finish(solved, decay, before, first, second, third, table, out, result, sent):
+    north, south = packed(total[1], up)
+    for d, message in enumerate((message_1, message_2, message_3), 1):
+        message[...] = jnp.where(row ^ d > row, north, south)
+
+
+def lat_finish(
+    solved, decay, before, first, second, third, ahead_1, ahead_2, ahead_3, table, out, result, sent
+):
     lons, bins = before.shape[0] // 2, before.shape[1]
     rows = out.shape[0]
     count = rows // lons
     row = lax.axis_index("lat") // 4
     up = table[3:4, :] > 0.5
-    one, two, three = ((ref[...], pltpu.roll(ref[...], bins - HALF, 1)) for ref in (first, second, third))
-    entering = jnp.zeros_like(one[0])
-    for d, low, high in ((3, three, one), (2, two, two), (1, one, three)):
-        a, b = (jnp.where(up, x, y) for x, y in zip(low, high))
-        reached = jnp.where(up, (row >= d).astype(jnp.float32), (row < 4 - d).astype(jnp.float32))
+    received = [
+        [unpacked(a[...]), unpacked(b[...])]
+        for a, b in zip((ahead_1, ahead_2, ahead_3), (first, second, third))
+    ]
+
+    def from_row(source):
+        value = received[0]
+        for d in (2, 3):
+            value = [jnp.where(row ^ source == d, new, old) for new, old in zip(received[d - 1], value)]
+        return value
+
+    entering = jnp.zeros_like(received[0][0])
+    for n in range(3):
+        a, b = (jnp.where(up, x, y) for x, y in zip(from_row(n), from_row(3 - n)))
+        reached = jnp.where(up, (n < row).astype(jnp.float32), (3 - n > row).astype(jnp.float32))
         entering = jnp.where(reached > 0.5, a * entering + b, entering)
     entering = before[0:lons] * entering + before[lons : 2 * lons]
     copies = []
@@ -269,17 +319,16 @@
     )(*operands)
 
 
-def exchange(value, axis, near):
-    def route(d):
-        pairs = []
-        for i in range(16):
-            base, k = (i - i % 4, i % 4) if near else (i % 4, i // 4)
-            source = (k - d) % 4
-            pairs.append((base + source if near else base + 4 * source, i))
-        return pairs
-
-    values = value if isinstance(value, list) else [value] * 3
-    return [lax.ppermute(item, axis, route(d)) for d, item in enumerate(values, 1)]
+NEAR = [[i ^ d for i in range(16)] for d in (1, 2, 3)]
+FAR = [[i ^ d for i in range(16)] for d in (4, 8, 12)]
+FAR_LON = [[i ^ d for i in range(16)] for d in (4, 10, 12)]
+
+
+def exchange(values, axis, sources):
+    return [
+        lax.ppermute(value, axis, [(source, i) for i, source in enumerate(places)])
+        for value, places in zip(values, sources)
+    ]
 
 
 def body(wave_action, lon_speed, lat_speed, land_mask, open_edges):
@@ -287,15 +336,15 @@
     table = jnp.asarray(bin_tables(bins))
     flat = (lons * lats, bins)
     wave, speed, lat_rate = (x.reshape(flat) for x in (wave_action, lon_speed, lat_speed))
-    small, large = (2 * lats, bins), (2 * lons, bins)
+    small, large = (lats, bins), (2 * lons, bins)
 
     tiled = (bins // LANES * lons * lats, LANES)
     buffer = pltpu.VMEM(tiled, jnp.float32)
     signals = pltpu.SemaphoreType.DMA((bins // LANES,))
 
     sea = land_mask.T
-    own, partial, decay = run(
-        lon_local, [small, tiled, tiled], wave, speed, sea, table,
+    keep, give, partial, decay = run(
+        lon_local, [small, small, tiled, tiled], wave, speed, sea, table,
         scratch=[
             pltpu.VMEM(flat, jnp.float32), pltpu.VMEM(flat, jnp.float32),
             pltpu.VMEM(sea.shape, sea.dtype), pltpu.VMEM(table.shape, table.dtype),
@@ -303,22 +352,34 @@
         ],
         far_inputs=range(4),
     )
-    near = exchange(own, "lon", True)
-    ratio, scaled, lat_decay = run(
-        lat_coefficients, [tiled] * 3, lat_rate, sea, open_edges, table, scratch=[buffer]
-    )
-    whole, before = run(lon_group, [small, small], own, *near, table)
-    far = exchange(whole, "lon", False)
+    near = exchange([give, keep, give], "lon", NEAR)
+    ratio, scaled, lat_decay, lat_ahead = run(
+        lat_coefficients, [tiled] * 3 + [(lons, bins)], lat_rate, sea, open_edges, table,
+        scratch=[buffer],
+    )
+    near_ahead = exchange([lat_ahead] * 3, "lat", NEAR)
+    whole, before, before_partner = run(lon_group, [small] * 3, keep, *near, table)
+    far = exchange([whole] * 3, "lon", FAR_LON)
+    half = (lons // 2, bins)
+    far_ahead = exchange(
+        run(lat_group_ahead, [half] * 3, lat_ahead, *near_ahead, table), "lat", FAR
+    )
+    inflow = (lats // 2, bins)
+    kept, give = run(
+        lon_cycle, [inflow, inflow], whole, *far, before, before_partner, table
+    )
+    given = lax.ppermute(give, "lon", [(i ^ 1, i) for i in range(16)])
     lat_own, solved = run(
-        lon_finish, [large, tiled],
-        partial, decay, whole, *far, before, ratio, scaled, lat_decay, table,
+        lon_finish, [(lons, bins), tiled], partial, decay, kept, given, ratio, scaled, table,
         scratch=[buffer],
     )
-    near = exchange(lat_own, "lat", True)
-    lat_before, *sends = run(lat_group, [large, *[(lons, bins)] * 3], lat_own, *near, table)
-    far = exchange(list(sends), "lat", False)
+    near = exchange([lat_own] * 3, "lat", NEAR)
+    lat_before, *sends = run(
+        lat_group, [large, *[half] * 3], lat_own, lat_ahead, *near, *near_ahead, table
+    )
+    far = exchange(sends, "lat", FAR)
     (out,) = run(
-        lat_finish, [flat], solved, lat_decay, lat_before, *far, table,
+        lat_finish, [flat], solved, lat_decay, lat_before, *far, *far_ahead, table,
         scratch=[buffer, signals], far_outputs=(0,),
     )
     return out.reshape(wave_action.shape)

time: 44.9 us -> 43.1 us (0.960)
  the two profiles are of different devices: /device:TPU:24 before, /device:TPU:4 now
where the time goes in v3:
time: 43.1 us; the launch traced here: 43 us
  starting transfers between devices  27 us (63%)
  waiting for transfers between devices  11.6 us (27%)
  Pallas kernels  3.8 us (9%)
  local copies, waits for them, and re-layouts  0.46 us (1%)
    ppermute x18, starting transfers between devices, exchange(): lax.ppermute(value, axis, [(source, i) for i, source in enumerate(places)])  26.9 us
    ppermute x18, waiting for transfers between devices, exchange(): lax.ppermute(value, axis, [(source, i) for i, source in enumerate(places)])  10.4 us
    pallas_call x8, Pallas kernels, run(): pl.pallas_call(kernel, out_shape=[jax.ShapeDtypeStruct(shape, jnp.float32...  3.8 us
    ppermute x1, waiting for transfers between devices, body(): given = lax.ppermute(give, 'lon', [(i ^ 1, i) for i in range(16)])  1.17 us
  transfers between devices with their start and end apart: 19, of which 6 were waited for; matrix products, arithmetic and copies ran while one was open for 0% of the time, Pallas kernels for 3%

profile of v3, /device:TPU:4, one launch (start us, length us, event | category | flops | bytes accessed | tf_op | source)
XLA Modules:
  0.0 43.0 jit_solution(14831759435887516026)
XLA Ops:
  0.0 1.6 %lon_local.1 = (f32[8,1152]{1,0:T(8,128)S(1)}, f32[8,1152]{1,0:T(8,128)S(1)}, f32[1152,128]{1,0:T(8,128)S(1)}, f32[1152,128]{1,0:T(8,128)S(1)}) custom-call(f32[128,1152]{1,0:T(8,128)} %bitcast.8, f32[128,1152]{1,0:T(8,128)} %bitcast.9, s32[8,16]{1,0:T(8,128)} %bitcast.6, f32[8,1152]{1,0:T(8,128)} %constant.2.clone.table_far.table.rest_3_), custom_call_target="tpu_custom_call" | custom-call | tf_op jit(solution)/shard_map/lon_local/pallas_call | solution.py:311
  1.6 2.0 %collective-permute-start.1 = (f32[8,1152]{1,0:T(8,128)S(1)}, f32[8,1152]{1,0:T(8,128)S(1)}, u32[]{:S(2)}, u32[]{:S(2)}) collective-permute-start(f32[8,1152]{1,0:T(8,128)S(1)} %get-tuple-element.29.own), channel_id=1, source_target_pairs={{32,0},{48,16},{0,32},{16,48},{96,64},{112,80},{64,96},{80,112},{1... | collective-permute-start | bytes 110600 | tf_op jit(solution)/shard_map/ppermute | solution.py:329
  3.9 0.4 %copy-done.3 = s32[2,16]{1,0:T(2,128)S(1)} copy-done((s32[2,16]{1,0:T(2,128)S(1)}, s32[2,16]{1,0:T(2,128)}, u32[]{:S(2)}) %copy-start.3) | copy-done | bytes 152
  4.3 0.4 lat_coefficients.1
  4.7 0.6 %collective-permute-start.12 = (f32[16,1152]{1,0:T(8,128)S(1)}, f32[16,1152]{1,0:T(8,128)S(1)}, u32[]{:S(2)}, u32[]{:S(2)}) collective-permute-start(f32[16,1152]{1,0:T(8,128)S(1)} %get-tuple-element.41.own_ahead.own), channel_id=1, source_target_pairs={{3,0},{2,1},{1,2},{0,3},{7,4},{6,5},{5,6},{4,7},{11,8},{10,9},{9,1... | collective-permute-start | bytes 221192 | tf_op jit(solution)/shard_map/ppermute | solution.py:329
  5.3 0.4 collective-permute-done.1.second
  5.7 1.5 %collective-permute-done.2.third = f32[8,1152]{1,0:T(8,128)S(1)} collective-permute-done((f32[8,1152]{1,0:T(8,128)S(1)}, f32[8,1152]{1,0:T(8,128)S(1)}, u32[]{:S(2)}, u32[]{:S(2)}) %collective-permute-start.2) | collective-permute-done | bytes 36896 | tf_op jit(solution)/shard_map/ppermute | solution.py:329
  7.3 5.7 %collective-permute-start.5 = (f32[8,1152]{1,0:T(8,128)S(1)}, f32[8,1152]{1,0:T(8,128)S(1)}, u32[]{:S(2)}, u32[]{:S(2)}) collective-permute-start(f32[8,1152]{1,0:T(8,128)S(1)} %get-tuple-element.31.own), channel_id=1, source_target_pairs={{192,0},{208,16},{224,32},{240,48},{128,64},{144,80},{160,96},{176... | collective-permute-start | bytes 110600 | tf_op jit(solution)/shard_map/ppermute | solution.py:329
  13.0 0.5 %collective-permute-start.4 = (f32[8,1152]{1,0:T(8,128)S(1)}, f32[8,1152]{1,0:T(8,128)S(1)}, u32[]{:S(2)}, u32[]{:S(2)}) collective-permute-start(f32[8,1152]{1,0:T(8,128)S(1)} %get-tuple-element.31.own), channel_id=1, source_target_pairs={{160,0},{176,16},{128,32},{144,48},{224,64},{240,80},{192,96},{208... | collective-permute-start | bytes 110600 | tf_op jit(solution)/shard_map/ppermute | solution.py:329
  13.5 1.5 %collective-permute-start.3 = (f32[8,1152]{1,0:T(8,128)S(1)}, f32[8,1152]{1,0:T(8,128)S(1)}, u32[]{:S(2)}, u32[]{:S(2)}) collective-permute-start(f32[8,1152]{1,0:T(8,128)S(1)} %get-tuple-element.31.own), channel_id=1, source_target_pairs={{64,0},{80,16},{96,32},{112,48},{0,64},{16,80},{32,96},{48,112},{1... | collective-permute-start | bytes 110600 | tf_op jit(solution)/shard_map/ppermute | solution.py:329
  15.0 1.2 %collective-permute-start.11 = (f32[16,1152]{1,0:T(8,128)S(1)}, f32[16,1152]{1,0:T(8,128)S(1)}, u32[]{:S(2)}, u32[]{:S(2)}) collective-permute-start(f32[16,1152]{1,0:T(8,128)S(1)} %get-tuple-element.41.own_ahead.own), channel_id=1, source_target_pairs={{2,0},{3,1},{0,2},{1,3},{6,4},{7,5},{4,6},{5,7},{10,8},{11,9},{8,1... | collective-permute-start | bytes 221192 | tf_op jit(solution)/shard_map/ppermute | solution.py:329
  16.2 1.4 %collective-permute-start.10 = (f32[16,1152]{1,0:T(8,128)S(1)}, f32[16,1152]{1,0:T(8,128)S(1)}, u32[]{:S(2)}, u32[]{:S(2)}) collective-permute-start(f32[16,1152]{1,0:T(8,128)S(1)} %get-tuple-element.41.own_ahead.own), channel_id=1, source_target_pairs={{1,0},{0,1},{3,2},{2,3},{5,4},{4,5},{7,6},{6,7},{9,8},{8,9},{11,10... | collective-permute-start | bytes 221192 | tf_op jit(solution)/shard_map/ppermute | solution.py:329
  17.6 3.6 %collective-permute-done.4.second = f32[8,1152]{1,0:T(8,128)S(1)} collective-permute-done((f32[8,1152]{1,0:T(8,128)S(1)}, f32[8,1152]{1,0:T(8,128)S(1)}, u32[]{:S(2)}, u32[]{:S(2)}) %collective-permute-start.4) | collective-permute-done | bytes 36896 | tf_op jit(solution)/shard_map/ppermute | solution.py:329
  21.4 1.2 %collective-permute-done.6.given = f32[4,1152]{1,0:T(4,128)S(1)} collective-permute-done((f32[4,1152]{1,0:T(4,128)S(1)}, f32[4,1152]{1,0:T(4,128)S(1)}, u32[]{:S(2)}, u32[]{:S(2)}) %collective-permute-start.6) | collective-permute-done | bytes 18464 | tf_op jit(solution)/shard_map/ppermute | solution.py:371
  22.9 0.6 %collective-permute-start.9 = (f32[16,1152]{1,0:T(8,128)S(1)}, f32[16,1152]{1,0:T(8,128)S(1)}, u32[]{:S(2)}, u32[]{:S(2)}) collective-permute-start(f32[16,1152]{1,0:T(8,128)S(1)} %get-tuple-element.40.own), channel_id=1, source_target_pairs={{3,0},{2,1},{1,2},{0,3},{7,4},{6,5},{5,6},{4,7},{11,8},{10,9},{9,1... | collective-permute-start | bytes 221192 | tf_op jit(solution)/shard_map/ppermute | solution.py:329
  23.5 2.7 %collective-permute-start.8 = (f32[16,1152]{1,0:T(8,128)S(1)}, f32[16,1152]{1,0:T(8,128)S(1)}, u32[]{:S(2)}, u32[]{:S(2)}) collective-permute-start(f32[16,1152]{1,0:T(8,128)S(1)} %get-tuple-element.40.own), channel_id=1, source_target_pairs={{2,0},{3,1},{0,2},{1,3},{6,4},{7,5},{4,6},{5,7},{10,8},{11,9},{8,1... | collective-permute-start | bytes 221192 | tf_op jit(solution)/shard_map/ppermute | solution.py:329
  26.2 0.8 %collective-permute-start.7 = (f32[16,1152]{1,0:T(8,128)S(1)}, f32[16,1152]{1,0:T(8,128)S(1)}, u32[]{:S(2)}, u32[]{:S(2)}) collective-permute-start(f32[16,1152]{1,0:T(8,128)S(1)} %get-tuple-element.40.own), channel_id=1, source_target_pairs={{1,0},{0,1},{3,2},{2,3},{5,4},{4,5},{7,6},{6,7},{9,8},{8,9},{11,10... | collective-permute-start | bytes 221192 | tf_op jit(solution)/shard_map/ppermute | solution.py:329
  27.2 1.7 %collective-permute-start.16 = (f32[8,1152]{1,0:T(8,128)S(1)}, f32[8,1152]{1,0:T(8,128)S(1)}, u32[]{:S(2)}, u32[]{:S(2)}) collective-permute-start(f32[8,1152]{1,0:T(8,128)S(1)} %get-tuple-element.46), channel_id=1, source_target_pairs={{4,0},{5,1},{6,2},{7,3},{0,4},{1,5},{2,6},{3,7},{12,8},{13,9},{14,... | collective-permute-start | bytes 110600 | tf_op jit(solution)/shard_map/ppermute | solution.py:329
  28.8 2.9 %collective-permute-start.17 = (f32[8,1152]{1,0:T(8,128)S(1)}, f32[8,1152]{1,0:T(8,128)S(1)}, u32[]{:S(2)}, u32[]{:S(2)}) collective-permute-start(f32[8,1152]{1,0:T(8,128)S(1)} %get-tuple-element.47), channel_id=1, source_target_pairs={{8,0},{9,1},{10,2},{11,3},{12,4},{13,5},{14,6},{15,7},{0,8},{1,9},... | collective-permute-start | bytes 110600 | tf_op jit(solution)/shard_map/ppermute | solution.py:329
  32.2 0.5 %collective-permute-start.13 = (f32[8,1152]{1,0:T(8,128)S(1)}, f32[8,1152]{1,0:T(8,128)S(1)}, u32[]{:S(2)}, u32[]{:S(2)}) collective-permute-start(f32[8,1152]{1,0:T(8,128)S(1)} %get-tuple-element.43), channel_id=1, source_target_pairs={{4,0},{5,1},{6,2},{7,3},{0,4},{1,5},{2,6},{3,7},{12,8},{13,9},{14,... | collective-permute-start | bytes 110600 | tf_op jit(solution)/shard_map/ppermute | solution.py:329
  32.7 4.1 %collective-permute-start.14 = (f32[8,1152]{1,0:T(8,128)S(1)}, f32[8,1152]{1,0:T(8,128)S(1)}, u32[]{:S(2)}, u32[]{:S(2)}) collective-permute-start(f32[8,1152]{1,0:T(8,128)S(1)} %get-tuple-element.44), channel_id=1, source_target_pairs={{8,0},{9,1},{10,2},{11,3},{12,4},{13,5},{14,6},{15,7},{0,8},{1,9},... | collective-permute-start | bytes 110600 | tf_op jit(solution)/shard_map/ppermute | solution.py:329
  37.0 2.2 %collective-permute-done.14.second = f32[8,1152]{1,0:T(8,128)S(1)} collective-permute-done((f32[8,1152]{1,0:T(8,128)S(1)}, f32[8,1152]{1,0:T(8,128)S(1)}, u32[]{:S(2)}, u32[]{:S(2)}) %collective-permute-start.14) | collective-permute-done | bytes 36896 | tf_op jit(solution)/shard_map/ppermute | solution.py:329
  39.2 2.7 %collective-permute-done.15.third = f32[8,1152]{1,0:T(8,128)S(1)} collective-permute-done((f32[8,1152]{1,0:T(8,128)S(1)}, f32[8,1152]{1,0:T(8,128)S(1)}, u32[]{:S(2)}, u32[]{:S(2)}) %collective-permute-start.15) | collective-permute-done | bytes 36896 | tf_op jit(solution)/shard_map/ppermute | solution.py:329
  41.9 1.0 %lat_finish.1 = f32[128,1152]{1,0:T(8,128)} custom-call(f32[1152,128]{1,0:T(8,128)S(1)} %get-tuple-element.38.solved, f32[1152,128]{1,0:T(8,128)S(1)} %get-tuple-element.39.decay, f32[32,1152]{1,0:T(8,128)S(1)} %get-tuple-element.42.before, f32[8,1152]{1,0:T(8,128)S(1)} %collective-permute-done.13.first, f32[8,1152]{1,0:T(8,128)S(1)} %collective-permute-done.14.second, ...), custom_call_target="tpu_custom_call" | custom-call | tf_op jit(solution)/shard_map/lat_finish/pallas_call | solution.py:311
  (30 shorter events, 1.6 us)
Async XLA Ops:
  0.0 3.9 %copy-start = (f32[8,1152]{1,0:T(8,128)S(1)}, f32[8,1152]{1,0:T(8,128)}, u32[]{:S(2)}) copy-start(f32[8,1152]{1,0:T(8,128)} %constant.2.clone.table_far.table.rest_3_) | copy-start | bytes 110596
  0.0 3.9 %copy-start.1 = (f32[16,8,1152]{2,1,0:T(8,128)S(1)}, f32[16,8,1152]{2,1,0:T(8,128)}, u32[]{:S(2)}) copy-start(f32[16,8,1152]{2,1,0:T(8,128)} %param.8) | copy-start | bytes 1769476
  1.6 2.3 %copy-start.2 = (s32[16,8]{0,1:T(8,128)S(1)}, s32[16,8]{0,1:T(8,128)}, u32[]{:S(2)}) copy-start(s32[16,8]{0,1:T(8,128)} %param.9) | copy-start | bytes 1540
  1.6 4.0 %collective-permute-start.1 = (f32[8,1152]{1,0:T(8,128)S(1)}, f32[8,1152]{1,0:T(8,128)S(1)}, u32[]{:S(2)}, u32[]{:S(2)}) collective-permute-start(f32[8,1152]{1,0:T(8,128)S(1)} %get-tuple-element.29.own), channel_id=1, source_target_pairs={{32,0},{48,16},{0,32},{16,48},{96,64},{112,80},{64,96},{80,112},{1... | collective-permute-start | bytes 110600 | tf_op jit(solution)/shard_map/ppermute | solution.py:329
  3.6 0.7 %copy-start.3 = (s32[2,16]{1,0:T(2,128)S(1)}, s32[2,16]{1,0:T(2,128)}, u32[]{:S(2)}) copy-start(s32[2,16]{1,0:T(2,128)} %edges.1) | copy-start | bytes 388
  3.6 3.5 %collective-permute-start.2 = (f32[8,1152]{1,0:T(8,128)S(1)}, f32[8,1152]{1,0:T(8,128)S(1)}, u32[]{:S(2)}, u32[]{:S(2)}) collective-permute-start(f32[8,1152]{1,0:T(8,128)S(1)} %get-tuple-element.30), channel_id=1, source_target_pairs={{48,0},{32,16},{16,32},{0,48},{112,64},{96,80},{80,96},{64,112},{1... | collective-permute-start | bytes 110600 | tf_op jit(solution)/shard_map/ppermute | solution.py:329
  3.6 3.5 %collective-permute-start = (f32[8,1152]{1,0:T(8,128)S(1)}, f32[8,1152]{1,0:T(8,128)S(1)}, u32[]{:S(2)}, u32[]{:S(2)}) collective-permute-start(f32[8,1152]{1,0:T(8,128)S(1)} %get-tuple-element.30), channel_id=1, source_target_pairs={{16,0},{0,16},{48,32},{32,48},{80,64},{64,80},{112,96},{96,112},{1... | collective-permute-start | bytes 110600 | tf_op jit(solution)/shard_map/ppermute | solution.py:329
  4.7 21.6 %collective-permute-start.12 = (f32[16,1152]{1,0:T(8,128)S(1)}, f32[16,1152]{1,0:T(8,128)S(1)}, u32[]{:S(2)}, u32[]{:S(2)}) collective-permute-start(f32[16,1152]{1,0:T(8,128)S(1)} %get-tuple-element.41.own_ahead.own), channel_id=1, source_target_pairs={{3,0},{2,1},{1,2},{0,3},{7,4},{6,5},{5,6},{4,7},{11,8},{10,9},{9,1... | collective-permute-start | bytes 221192 | tf_op jit(solution)/shard_map/ppermute | solution.py:329
  7.3 8.9 %collective-permute-start.5 = (f32[8,1152]{1,0:T(8,128)S(1)}, f32[8,1152]{1,0:T(8,128)S(1)}, u32[]{:S(2)}, u32[]{:S(2)}) collective-permute-start(f32[8,1152]{1,0:T(8,128)S(1)} %get-tuple-element.31.own), channel_id=1, source_target_pairs={{192,0},{208,16},{224,32},{240,48},{128,64},{144,80},{160,96},{176... | collective-permute-start | bytes 110600 | tf_op jit(solution)/shard_map/ppermute | solution.py:329
  13.0 8.2 %collective-permute-start.4 = (f32[8,1152]{1,0:T(8,128)S(1)}, f32[8,1152]{1,0:T(8,128)S(1)}, u32[]{:S(2)}, u32[]{:S(2)}) collective-permute-start(f32[8,1152]{1,0:T(8,128)S(1)} %get-tuple-element.31.own), channel_id=1, source_target_pairs={{160,0},{176,16},{128,32},{144,48},{224,64},{240,80},{192,96},{208... | collective-permute-start | bytes 110600 | tf_op jit(solution)/shard_map/ppermute | solution.py:329
  13.5 7.7 %collective-permute-start.3 = (f32[8,1152]{1,0:T(8,128)S(1)}, f32[8,1152]{1,0:T(8,128)S(1)}, u32[]{:S(2)}, u32[]{:S(2)}) collective-permute-start(f32[8,1152]{1,0:T(8,128)S(1)} %get-tuple-element.31.own), channel_id=1, source_target_pairs={{64,0},{80,16},{96,32},{112,48},{0,64},{16,80},{32,96},{48,112},{1... | collective-permute-start | bytes 110600 | tf_op jit(solution)/shard_map/ppermute | solution.py:329
  15.0 12.1 %collective-permute-start.11 = (f32[16,1152]{1,0:T(8,128)S(1)}, f32[16,1152]{1,0:T(8,128)S(1)}, u32[]{:S(2)}, u32[]{:S(2)}) collective-permute-start(f32[16,1152]{1,0:T(8,128)S(1)} %get-tuple-element.41.own_ahead.own), channel_id=1, source_target_pairs={{2,0},{3,1},{0,2},{1,3},{6,4},{7,5},{4,6},{5,7},{10,8},{11,9},{8,1... | collective-permute-start | bytes 221192 | tf_op jit(solution)/shard_map/ppermute | solution.py:329
  16.2 10.9 %collective-permute-start.10 = (f32[16,1152]{1,0:T(8,128)S(1)}, f32[16,1152]{1,0:T(8,128)S(1)}, u32[]{:S(2)}, u32[]{:S(2)}) collective-permute-start(f32[16,1152]{1,0:T(8,128)S(1)} %get-tuple-element.41.own_ahead.own), channel_id=1, source_target_pairs={{1,0},{0,1},{3,2},{2,3},{5,4},{4,5},{7,6},{6,7},{9,8},{8,9},{11,10... | collective-permute-start | bytes 221192 | tf_op jit(solution)/shard_map/ppermute | solution.py:329
  21.3 1.3 %collective-permute-start.6 = (f32[4,1152]{1,0:T(4,128)S(1)}, f32[4,1152]{1,0:T(4,128)S(1)}, u32[]{:S(2)}, u32[]{:S(2)}) collective-permute-start(f32[4,1152]{1,0:T(4,128)S(1)} %get-tuple-element.35), channel_id=1, source_target_pairs={{16,0},{0,16},{48,32},{32,48},{80,64},{64,80},{112,96},{96,112},{1... | collective-permute-start | bytes 55304 | tf_op jit(solution)/shard_map/ppermute | solution.py:371
  22.9 8.9 %collective-permute-start.9 = (f32[16,1152]{1,0:T(8,128)S(1)}, f32[16,1152]{1,0:T(8,128)S(1)}, u32[]{:S(2)}, u32[]{:S(2)}) collective-permute-start(f32[16,1152]{1,0:T(8,128)S(1)} %get-tuple-element.40.own), channel_id=1, source_target_pairs={{3,0},{2,1},{1,2},{0,3},{7,4},{6,5},{5,6},{4,7},{11,8},{10,9},{9,1... | collective-permute-start | bytes 221192 | tf_op jit(solution)/shard_map/ppermute | solution.py:329
  23.5 8.5 %collective-permute-start.8 = (f32[16,1152]{1,0:T(8,128)S(1)}, f32[16,1152]{1,0:T(8,128)S(1)}, u32[]{:S(2)}, u32[]{:S(2)}) collective-permute-start(f32[16,1152]{1,0:T(8,128)S(1)} %get-tuple-element.40.own), channel_id=1, source_target_pairs={{2,0},{3,1},{0,2},{1,3},{6,4},{7,5},{4,6},{5,7},{10,8},{11,9},{8,1... | collective-permute-start | bytes 221192 | tf_op jit(solution)/shard_map/ppermute | solution.py:329
  26.2 5.7 %collective-permute-start.7 = (f32[16,1152]{1,0:T(8,128)S(1)}, f32[16,1152]{1,0:T(8,128)S(1)}, u32[]{:S(2)}, u32[]{:S(2)}) collective-permute-start(f32[16,1152]{1,0:T(8,128)S(1)} %get-tuple-element.40.own), channel_id=1, source_target_pairs={{1,0},{0,1},{3,2},{2,3},{5,4},{4,5},{7,6},{6,7},{9,8},{8,9},{11,10... | collective-permute-start | bytes 221192 | tf_op jit(solution)/shard_map/ppermute | solution.py:329
  27.2 9.6 %collective-permute-start.16 = (f32[8,1152]{1,0:T(8,128)S(1)}, f32[8,1152]{1,0:T(8,128)S(1)}, u32[]{:S(2)}, u32[]{:S(2)}) collective-permute-start(f32[8,1152]{1,0:T(8,128)S(1)} %get-tuple-element.46), channel_id=1, source_target_pairs={{4,0},{5,1},{6,2},{7,3},{0,4},{1,5},{2,6},{3,7},{12,8},{13,9},{14,... | collective-permute-start | bytes 110600 | tf_op jit(solution)/shard_map/ppermute | solution.py:329
  28.8 8.1 %collective-permute-start.17 = (f32[8,1152]{1,0:T(8,128)S(1)}, f32[8,1152]{1,0:T(8,128)S(1)}, u32[]{:S(2)}, u32[]{:S(2)}) collective-permute-start(f32[8,1152]{1,0:T(8,128)S(1)} %get-tuple-element.47), channel_id=1, source_target_pairs={{8,0},{9,1},{10,2},{11,3},{12,4},{13,5},{14,6},{15,7},{0,8},{1,9},... | collective-permute-start | bytes 110600 | tf_op jit(solution)/shard_map/ppermute | solution.py:329
  31.7 5.2 %collective-permute-start.18 = (f32[8,1152]{1,0:T(8,128)S(1)}, f32[8,1152]{1,0:T(8,128)S(1)}, u32[]{:S(2)}, u32[]{:S(2)}) collective-permute-start(f32[8,1152]{1,0:T(8,128)S(1)} %get-tuple-element.48), channel_id=1, source_target_pairs={{12,0},{13,1},{14,2},{15,3},{8,4},{9,5},{10,6},{11,7},{4,8},{5,9},... | collective-permute-start | bytes 110600 | tf_op jit(solution)/shard_map/ppermute | solution.py:329
  32.2 4.8 %collective-permute-start.13 = (f32[8,1152]{1,0:T(8,128)S(1)}, f32[8,1152]{1,0:T(8,128)S(1)}, u32[]{:S(2)}, u32[]{:S(2)}) collective-permute-start(f32[8,1152]{1,0:T(8,128)S(1)} %get-tuple-element.43), channel_id=1, source_target_pairs={{4,0},{5,1},{6,2},{7,3},{0,4},{1,5},{2,6},{3,7},{12,8},{13,9},{14,... | collective-permute-start | bytes 110600 | tf_op jit(solution)/shard_map/ppermute | solution.py:329
  32.7 6.5 %collective-permute-start.14 = (f32[8,1152]{1,0:T(8,128)S(1)}, f32[8,1152]{1,0:T(8,128)S(1)}, u32[]{:S(2)}, u32[]{:S(2)}) collective-permute-start(f32[8,1152]{1,0:T(8,128)S(1)} %get-tuple-element.44), channel_id=1, source_target_pairs={{8,0},{9,1},{10,2},{11,3},{12,4},{13,5},{14,6},{15,7},{0,8},{1,9},... | collective-permute-start | bytes 110600 | tf_op jit(solution)/shard_map/ppermute | solution.py:329
  36.8 5.2 %collective-permute-start.15 = (f32[8,1152]{1,0:T(8,128)S(1)}, f32[8,1152]{1,0:T(8,128)S(1)}, u32[]{:S(2)}, u32[]{:S(2)}) collective-permute-start(f32[8,1152]{1,0:T(8,128)S(1)} %get-tuple-element.45), channel_id=1, source_target_pairs={{12,0},{13,1},{14,2},{15,3},{8,4},{9,5},{10,6},{11,7},{4,8},{5,9},... | collective-permute-start | bytes 110600 | tf_op jit(solution)/shard_map/ppermute | solution.py:329
